TPU v7x, 32 devices: a whole 2x2x4 slice. The times are simulated.
32 devices in a mesh: dp: 2 (over x), cfg: 4 (over z), tp: 4 (over y, core).
Axes of the slice: x: 2, y: 2, z: 4, core: 2. Of those that a mesh axis runs over, the one named last changes fastest.
Arguments:
- hidden: bfloat16 [32, 1024, 1152], P(('dp', 'cfg')), parts along dimension 0
- caption: bfloat16 [32, 300, 1152], P(('dp', 'cfg')), parts along dimension 0
- cap_len: int32 [32], P(('dp', 'cfg')), parts along dimension 0
- t_block: bfloat16 [16, 6912], P('dp'), parts along dimension 0
- t_embed: bfloat16 [16, 1152], P('dp'), parts along dimension 0
- x_t: float32 [16, 64, 64, 4], P('dp'), parts along dimension 0
- alpha_bar: float32 [16, 2], P('dp'), parts along dimension 0
- mod_table: bfloat16 [2, 6, 1152], replicated
- w_qkv: bfloat16 [2, 1152, 3, 16, 72], P(None, None, None, 'tp')
- w_proj: bfloat16 [2, 16, 72, 1152], P(None, 'tp')
- w_cq: bfloat16 [2, 1152, 16, 72], P(None, None, 'tp')
- w_ckv: bfloat16 [2, 1152, 2, 16, 72], P(None, None, None, 'tp')
- w_cproj: bfloat16 [2, 16, 72, 1152], P(None, 'tp')
- w_fc1: bfloat16 [2, 1152, 4608], P(None, None, 'tp')
- w_fc2: bfloat16 [2, 4608, 1152], P(None, 'tp')
- final_table: bfloat16 [2, 1152], replicated
- w_out: bfloat16 [1152, 32], replicated
- b_out: bfloat16 [32], replicated
Outputs:
- output: float32 [16, 64, 64, 4], P('dp'), parts along dimension 0
There are 2 independent parts. A program takes and returns all parts, laid end to end along the dimension named above; an argument that names none is the same for every part.
All inputs are finite; a program needn't handle non-finite values.
Results may differ from a plain program's by a relative error of at most 0.0137388.
Values are sent between devices in bfloat16 or wider.
A program may use at most 1 GiB of HBM per device.

v0:
```python
import jax
import jax.numpy as jnp
from jax import lax
from jax.sharding import PartitionSpec as P

GUIDANCE = 4.5
LN_EPS = 1e-6


def layer_norm(values):
    mean_val = jnp.mean(values, axis=-1, keepdims=True)
    centered = values - mean_val
    variance = jnp.mean(centered * centered, axis=-1, keepdims=True)
    return centered * lax.rsqrt(variance + LN_EPS)


def attention(queries, key_vecs, values, key_mask):
    qk_scale = queries.shape[-1] ** -0.5
    scores = jnp.einsum('rqhd,rkhd->rhqk', queries, key_vecs, preferred_element_type=jnp.float32) * qk_scale
    if key_mask is not None:
        scores = jnp.where(key_mask, scores, -1e30)
    attn_prob = jax.nn.softmax(scores, axis=-1).astype(jnp.bfloat16)
    return jnp.einsum('rhqk,rkhd->rqhd', attn_prob, values, preferred_element_type=jnp.float32).astype(jnp.bfloat16)


def tp_block(residual, caption, key_mask, mod_rows, w_qkv, w_proj, w_cq, w_ckv, w_cproj, w_fc1, w_fc2):
    attn_in = (layer_norm(residual) * (1.0 + mod_rows[:, None, 1]) + mod_rows[:, None, 0]).astype(jnp.bfloat16)
    qkv_out = jnp.einsum('rnd,dshe->rnshe', attn_in, w_qkv, preferred_element_type=jnp.float32).astype(jnp.bfloat16)
    self_o = attention(qkv_out[:, :, 0], qkv_out[:, :, 1], qkv_out[:, :, 2], None)
    self_part = jnp.einsum('rnhe,hed->rnd', self_o, w_proj, preferred_element_type=jnp.float32).astype(jnp.bfloat16)
    residual = residual + mod_rows[:, None, 2] * lax.psum(self_part, 'tp').astype(jnp.float32)
    cross_q = jnp.einsum('rnd,dhe->rnhe', residual.astype(jnp.bfloat16), w_cq, preferred_element_type=jnp.float32).astype(jnp.bfloat16)
    cross_kv = jnp.einsum('rtd,dshe->rtshe', caption, w_ckv, preferred_element_type=jnp.float32).astype(jnp.bfloat16)
    cross_o = attention(cross_q, cross_kv[:, :, 0], cross_kv[:, :, 1], key_mask)
    cross_part = jnp.einsum('rnhe,hed->rnd', cross_o, w_cproj, preferred_element_type=jnp.float32).astype(jnp.bfloat16)
    residual = residual + lax.psum(cross_part, 'tp').astype(jnp.float32)
    mlp_in = (layer_norm(residual) * (1.0 + mod_rows[:, None, 4]) + mod_rows[:, None, 3]).astype(jnp.bfloat16)
    mlp_hidden = jax.nn.gelu(jnp.einsum('rnd,df->rnf', mlp_in, w_fc1, preferred_element_type=jnp.float32), approximate=True).astype(jnp.bfloat16)
    mlp_part = jnp.einsum('rnf,fd->rnd', mlp_hidden, w_fc2, preferred_element_type=jnp.float32).astype(jnp.bfloat16)
    return residual + mod_rows[:, None, 5] * lax.psum(mlp_part, 'tp').astype(jnp.float32)


def final_layer(residual, final_table, emb_rows, w_out, b_out, side_len):
    shift_scale = final_table.astype(jnp.float32)[None] + emb_rows[:, None]
    final_in = (layer_norm(residual) * (1.0 + shift_scale[:, None, 1]) + shift_scale[:, None, 0]).astype(jnp.bfloat16)
    out_tok = jnp.einsum('rnd,dc->rnc', final_in, w_out, preferred_element_type=jnp.float32) + b_out.astype(jnp.float32)
    n_rows = residual.shape[0]
    grid_side = side_len // 2
    patches = out_tok.reshape(n_rows, grid_side, grid_side, 2, 2, 8)[:, :, :, :, :, :4]
    return patches.transpose(0, 1, 3, 2, 4, 5).reshape(n_rows, side_len, side_len, 4)


def guidance_mix(eps_all):
    n_images = eps_all.shape[0] // 2
    eps_uncond = eps_all[n_images:]
    return eps_uncond + GUIDANCE * (eps_all[:n_images] - eps_uncond)


def ddim_update(guided, x_t, alpha_bar):
    abar_t = alpha_bar[:, 0][:, None, None, None]
    abar_prev = alpha_bar[:, 1][:, None, None, None]
    x_zero = (x_t - jnp.sqrt(1.0 - abar_t) * guided) / jnp.sqrt(abar_t)
    return jnp.sqrt(abar_prev) * x_zero + jnp.sqrt(1.0 - abar_prev) * guided


def solution(mesh):
    row_spec = P(('dp', 'cfg'))
    part_spec = P('dp')
    in_specs = (row_spec, row_spec, row_spec, part_spec, part_spec, part_spec, part_spec, P(),
                P(None, None, None, 'tp'), P(None, 'tp'), P(None, None, 'tp'), P(None, None, None, 'tp'),
                P(None, 'tp'), P(None, None, 'tp'), P(None, 'tp'), P(), P(), P())

    def local_step(hidden, caption, cap_len, t_block, t_embed, x_t, alpha_bar, mod_table, w_qkv, w_proj, w_cq, w_ckv, w_cproj, w_fc1, w_fc2, final_table, w_out, b_out):
        n_rows = hidden.shape[0]
        model_dim = hidden.shape[2]
        row_start = (lax.axis_index('cfg') * n_rows) % t_block.shape[0]
        t_rows = lax.dynamic_slice_in_dim(t_block, row_start, n_rows, axis=0).astype(jnp.float32).reshape(n_rows, 6, model_dim)
        emb_rows = lax.dynamic_slice_in_dim(t_embed, row_start, n_rows, axis=0).astype(jnp.float32)
        key_mask = (jnp.arange(caption.shape[1])[None, :] < cap_len[:, None])[:, None, None, :]
        residual = hidden.astype(jnp.float32)
        for layer_idx in range(mod_table.shape[0]):
            mod_rows = mod_table[layer_idx].astype(jnp.float32)[None] + t_rows
            residual = tp_block(residual, caption, key_mask, mod_rows, w_qkv[layer_idx], w_proj[layer_idx], w_cq[layer_idx], w_ckv[layer_idx], w_cproj[layer_idx], w_fc1[layer_idx], w_fc2[layer_idx])
        eps_local = final_layer(residual, final_table, emb_rows, w_out, b_out, x_t.shape[1])
        eps_all = lax.all_gather(eps_local, 'cfg', axis=0, tiled=True)
        return ddim_update(guidance_mix(eps_all), x_t, alpha_bar)

    return jax.shard_map(local_step, mesh=mesh, in_specs=in_specs, out_specs=part_spec, check_vma=False)
```

profile of v0, /device:TPU:0, one launch (start us, length us, event | category | flops | bytes accessed | tf_op | source)
XLA Modules:
  0.0 1562.4 jit_solution(14969140194960857347)
XLA Ops:
  6.5 1.0 dynamic-slice_convert_fusion
  7.6 0.9 fusion.200
  8.5 0.7 broadcast_add_fusion
  9.2 0.7 fusion.199
  9.9 5.1 convert_reduce_fusion
  15.1 6.5 fusion.20
  21.6 14.1 fusion.97
  35.7 29.4 %fusion.201 = (f32[4,4,1024]{2,1,0:T(4,128)S(1)}, f32[4,4,1024,1024]{2,3,1,0:T(8,128)}) fusion(bf16[4,1024,3,4,72]{1,4,3,2,0:T(8,128)(2,1)} %fusion.97), kind=kOutput, calls=%fused_computation.248 | convolution fusion | flops 2466251776 | bytes 71892992 | tf_op jit(solution)/shard_map/sub | solution.py:22
  65.1 28.1 %bitcast_convert_fusion.3 = bf16[4,1024,1152]{2,1,0:T(8,128)(2,1)} fusion(f32[4,4,1024,1024]{2,3,1,0:T(8,128)} %get-tuple-element.32, f32[4,4,1024]{2,1,0:T(4,128)S(1)} %get-tuple-element.31, bf16[4,1024,3,4,72]{1,4,3,2,0:T(8,128)(2,1)} %fusion.97, bf16[2,4,72,1152]{3,2,1,0:T(8,128)(2,1)S(1)} %copy-done.19), kind=kOutput, calls=%fused_computation.52 | convolution fusion | flops 5173280768 | bytes 79634432 | tf_op jit(solution)/shard_map/rnhe,hed->rnd/dot_general | solution.py:30
  93.4 4.7 fusion.146
  98.1 167.6 %all-reduce.7.cloned.1.call-done = bf16[4,1024,1152]{2,1,0:T(8,128)(2,1)} async-done(((bf16[4,1024,1152]{2,1,0:T(8,128)(2,1)}), bf16[4,1024,1152]{2,1,0:T(8,128)(2,1)}) %all-reduce.7.cloned.1.call-update) | async-done | bytes 9437200 | tf_op jit(solution)/shard_map/psum | solution.py:31
  265.8 14.2 fusion.133
  280.0 24.6 %fusion.202 = (f32[4,4,1024]{2,1,0:T(4,128)S(1)}, f32[4,4,1024,300]{2,3,1,0:T(8,128)}) fusion(f32[4,4,1024,300]{2,3,1,0:T(8,128)} %fusion.133, pred[4,300]{1,0:T(4,128)(4,1)S(1)} %iota_compare_fusion), kind=kOutput, calls=%fused_computation.249 | output fusion | flops 29491500 | bytes 39388336 | tf_op jit(solution)/shard_map/sub | solution.py:22
  304.6 14.2 bitcast_convert_fusion.2
  319.0 169.8 %all-reduce.9.cloned.1.call-done = bf16[4,1024,1152]{2,1,0:T(8,128)(2,1)} async-done(((bf16[4,1024,1152]{2,1,0:T(8,128)(2,1)}), bf16[4,1024,1152]{2,1,0:T(8,128)(2,1)}) %all-reduce.9.cloned.1.call-update) | async-done | bytes 9437200 | tf_op jit(solution)/shard_map/psum | solution.py:36
  488.8 11.1 fusion.195
  499.9 0.7 copy-done.1
  500.6 10.5 multiply_reduce_fusion.5
  511.2 23.6 %fusion.42.clone.5 = bf16[4,1024,1152]{2,1,0:T(8,128)(2,1)} fusion(f32[4,1152]{1,0:T(4,128)S(1)} %bitcast.286, f32[4,1152]{1,0:T(4,128)S(1)} %bitcast.287, f32[4,1024]{1,0:T(4,128)S(1)} %add_rsqrt_fusion.3, f32[4,1024]{1,0:T(4,128)S(1)} %broadcast_multiply_fusion.3, bf16[2,1152,1152]{2,1,0:T(8,128)(2,1)} %param.31, ...), kind=kOutput, calls=%fused_computation.72.clone.clone.clone.2 | convolution fusion | flops 10966007808 | bytes 40491008 | tf_op jit(solution)/shard_map/rnd,df->rnf/dot_general | solution.py:38
  534.8 19.3 %convolution_convert_fusion.1 = bf16[4,1024,1152]{2,1,0:T(8,128)(2,1)} fusion(bf16[2,1152,1152]{2,1,0:T(8,128)(2,1)} %param.32, bf16[4,1024,1152]{2,1,0:T(8,128)(2,1)} %fusion.42.clone.5), kind=kOutput, calls=%fused_computation.70 | convolution fusion | flops 10876354560 | bytes 21528576 | tf_op jit(solution)/shard_map/rnf,fd->rnd/dot_general | solution.py:39
  554.2 0.7 fusion.198
  554.9 169.1 %all-reduce.11.cloned.1.call-done = bf16[4,1024,1152]{2,1,0:T(8,128)(2,1)} async-done(((bf16[4,1024,1152]{2,1,0:T(8,128)(2,1)}), bf16[4,1024,1152]{2,1,0:T(8,128)(2,1)}) %all-reduce.11.cloned.1.call-update) | async-done | bytes 9437200 | tf_op jit(solution)/shard_map/psum | solution.py:40
  724.0 20.4 %fusion.197 = (f32[4,1024]{1,0:T(4,128)S(1)}, f32[4,1024,1152]{2,1,0:T(8,128)}) fusion(bf16[4,1024,1152]{2,1,0:T(8,128)(2,1)} %all-reduce.11.cloned.1.call-done, f32[4,1152]{1,0:T(4,128)S(1)} %bitcast.281, bf16[4,1024,1152]{2,1,0:T(8,128)(2,1)} %all-reduce.9.cloned.1.call-done, bf16[4,1024,1152]{2,1,0:T(8,128)(2,1)} %all-reduce.7.cloned.1.call-done, ...), kind=kLoop, calls=%fused_computation.244 | loop fusion | flops 47181824 | bytes 56676352 | tf_op jit(solution)/shard_map/reduce_sum | solution.py:11
  744.4 8.4 multiply_reduce_fusion.4
  752.9 16.0 %fusion.100 = bf16[4,1024,3,4,72]{1,4,3,2,0:T(8,128)(2,1)} fusion(f32[4,1024,1152]{2,1,0:T(8,128)} %get-tuple-element.8, f32[4,1152]{1,0:T(4,128)S(1)} %bitcast.282, f32[4,1152]{1,0:T(4,128)S(1)} %bitcast.283, f32[4,1024]{1,0:T(4,128)S(1)} %add_rsqrt_fusion.2, f32[4,1024]{1,0:T(4,128)S(1)} %broadcast_multiply_fusion.2, bf16[2,1152,3,4,72]{1,4,3,2,0:T(8,128)(2,1)} %param.26), kind=kOutput, calls=%fused_computation.116 | convolution fusion | flops 8180858880 | bytes 28012544 | tf_op jit(solution)/shard_map/rnd,dshe->rnshe/dot_general | solution.py:28
  768.8 29.7 %fusion.203 = (f32[4,4,1024]{2,1,0:T(4,128)S(1)}, f32[4,4,1024,1024]{2,3,1,0:T(8,128)}) fusion(bf16[4,1024,3,4,72]{1,4,3,2,0:T(8,128)(2,1)} %fusion.100), kind=kOutput, calls=%fused_computation.250 | convolution fusion | flops 2466251776 | bytes 71892992 | tf_op jit(solution)/shard_map/sub | solution.py:22
  798.6 28.0 %bitcast_convert_fusion.1 = bf16[4,1024,1152]{2,1,0:T(8,128)(2,1)} fusion(f32[4,4,1024,1024]{2,3,1,0:T(8,128)} %get-tuple-element.36, f32[4,4,1024]{2,1,0:T(4,128)S(1)} %get-tuple-element.35, bf16[4,1024,3,4,72]{1,4,3,2,0:T(8,128)(2,1)} %fusion.100, bf16[2,4,72,1152]{3,2,1,0:T(8,128)(2,1)S(1)} %copy-done.20), kind=kOutput, calls=%fused_computation.50 | convolution fusion | flops 5173280768 | bytes 79634432 | tf_op jit(solution)/shard_map/rnhe,hed->rnd/dot_general | solution.py:30
  826.7 4.7 fusion.149
  831.4 165.1 %all-reduce.13.cloned.1.call-done = bf16[4,1024,1152]{2,1,0:T(8,128)(2,1)} async-done(((bf16[4,1024,1152]{2,1,0:T(8,128)(2,1)}), bf16[4,1024,1152]{2,1,0:T(8,128)(2,1)}) %all-reduce.13.cloned.1.call-update) | async-done | bytes 9437200 | tf_op jit(solution)/shard_map/psum | solution.py:31
  996.6 16.1 %fusion.125 = f32[4,4,1024,300]{2,3,1,0:T(8,128)} fusion(f32[4,1024,1152]{2,1,0:T(8,128)} %get-tuple-element.8, bf16[4,1024,1152]{2,1,0:T(8,128)(2,1)} %all-reduce.13.cloned.1.call-done, f32[4,1152]{1,0:T(4,128)S(1)} %bitcast.276, bf16[4,300,2,4,72]{1,4,3,2,0:T(8,128)(2,1)S(1)} %fusion.149, bf16[2,1152,4,72]{1,3,2,0:T(8,128)(2,1)S(1)} %copy-done.4), kind=kOutput, calls=%fused_computation.141 | convolution fusion | flops 3445751808 | bytes 49539072 | tf_op jit(solution)/shard_map/rqhd,rkhd->rhqk/dot_general | solution.py:19
  1012.6 24.6 %fusion.204 = (f32[4,4,1024]{2,1,0:T(4,128)S(1)}, f32[4,4,1024,300]{2,3,1,0:T(8,128)}) fusion(f32[4,4,1024,300]{2,3,1,0:T(8,128)} %fusion.125, pred[4,300]{1,0:T(4,128)(4,1)S(1)} %copy-done.16), kind=kOutput, calls=%fused_computation.251 | output fusion | flops 29491500 | bytes 39388336 | tf_op jit(solution)/shard_map/sub | solution.py:22
  1037.2 14.3 bitcast_convert_fusion
  1051.7 169.8 %all-reduce.15.cloned.1.call-done = bf16[4,1024,1152]{2,1,0:T(8,128)(2,1)} async-done(((bf16[4,1024,1152]{2,1,0:T(8,128)(2,1)}), bf16[4,1024,1152]{2,1,0:T(8,128)(2,1)}) %all-reduce.15.cloned.1.call-update) | async-done | bytes 9437200 | tf_op jit(solution)/shard_map/psum | solution.py:36
  1221.5 20.0 %fusion.196 = (f32[4,1024]{1,0:T(4,128)S(1)}, f32[4,1024,1152]{2,1,0:T(8,128)}) fusion(bf16[4,1024,1152]{2,1,0:T(8,128)(2,1)} %all-reduce.15.cloned.1.call-done, f32[4,1024,1152]{2,1,0:T(8,128)} %get-tuple-element.8, bf16[4,1024,1152]{2,1,0:T(8,128)(2,1)} %all-reduce.13.cloned.1.call-done, f32[4,1152]{1,0:T(4,128)S(1)} %bitcast.277), kind=kLoop, calls=%fused_computation.243 | loop fusion | flops 28307456 | bytes 56657920 | tf_op jit(solution)/shard_map/reduce_sum | solution.py:11
  1241.5 8.4 multiply_reduce_fusion.3
  1250.0 39.4 %convolution_convert_fusion = bf16[4,1024,1152]{2,1,0:T(8,128)(2,1)} fusion(f32[4,1024,1152]{2,1,0:T(8,128)} %get-tuple-element.6, f32[4,1152]{1,0:T(4,128)S(1)} %bitcast.284, f32[4,1152]{1,0:T(4,128)S(1)} %bitcast.285, f32[4,1024]{1,0:T(4,128)S(1)} %add_rsqrt_fusion.1, f32[4,1024]{1,0:T(4,128)S(1)} %broadcast_multiply_fusion.1, ...), kind=kOutput, calls=%fused_computation.69 | convolution fusion | flops 21814050816 | bytes 33689600 | tf_op jit(solution)/shard_map/rnf,fd->rnd/dot_general | solution.py:39
  1289.6 169.7 %all-reduce.17.cloned.1.call-done = bf16[4,1024,1152]{2,1,0:T(8,128)(2,1)} async-done(((bf16[4,1024,1152]{2,1,0:T(8,128)(2,1)}), bf16[4,1024,1152]{2,1,0:T(8,128)(2,1)}) %all-reduce.17.cloned.1.call-update) | async-done | bytes 9437200 | tf_op jit(solution)/shard_map/psum | solution.py:40
  1459.4 12.1 fusion.103
  1471.5 10.2 multiply_reduce_fusion.2
  1481.8 0.6 slice-done.10
  1482.4 7.6 fusion.156
  1489.9 0.7 reshape.142
  1490.6 0.1 slice.204
  1490.7 8.9 copy.77
  1499.7 6.1 copy.42
  1505.8 45.6 %all-gather.2.cloned.1.call-done = f32[16,64,64,4]{2,1,3,0:T(8,128)} async-done(((f32[4,64,64,4]{2,1,3,0:T(8,128)}), f32[16,64,64,4]{2,1,3,0:T(8,128)}) %all-gather.2.cloned.1.call-update) | async-done | bytes 1048592 | tf_op jit(solution)/shard_map/all_gather | solution.py:85
  1551.4 2.2 fusion.161
  1553.6 1.6 copy.44
  (113 shorter events, 0.9 us)
Async XLA Ops:
  6.5 1475.2 %copy-start = (bf16[1152,32]{0,1:T(8,128)(2,1)S(1)}, bf16[1152,32]{0,1:T(8,128)(2,1)}, u32[]{:S(2)}) copy-start(bf16[1152,32]{0,1:T(8,128)(2,1)} %param.34) | copy-start | bytes 221188
  6.5 15.1 slice-start
  6.5 259.2 %all-reduce.7.cloned.1.call-start = ((), (), s32[]{:S(2)}) async-start(), calls=%async_computation | async-start | bytes 18874368 | tf_op jit(solution)/shard_map/psum | solution.py:31
  9.9 11.7 slice-start.1
  15.1 6.5 slice-start.2
  35.7 29.4 %copy-start.19 = (bf16[2,4,72,1152]{3,2,1,0:T(8,128)(2,1)S(1)}, bf16[2,4,72,1152]{3,2,1,0:T(8,128)(2,1)}, u32[]{:S(2)}) copy-start(bf16[2,4,72,1152]{3,2,1,0:T(8,128)(2,1)} %param.27) | copy-start | bytes 3981316
  65.1 28.2 %copy-start.18 = (s32[4]{0:T(128)S(1)}, s32[4]{0:T(128)}, u32[]{:S(2)}) copy-start(s32[4]{0:T(128)} %param.20) | copy-start | bytes 52
  93.2 172.6 %copy-start.3 = (bf16[2,1152,4,72]{1,3,2,0:T(8,128)(2,1)S(1)}, bf16[2,1152,4,72]{1,3,2,0:T(8,128)(2,1)}, u32[]{:S(2)}) copy-start(bf16[2,1152,4,72]{1,3,2,0:T(8,128)(2,1)} %param.28) | copy-start | bytes 3981316
  93.2 395.6 %all-reduce.9.cloned.1.call-start = ((), (), s32[]{:S(2)}) async-start(), calls=%async_computation.1 | async-start | bytes 18874368 | tf_op jit(solution)/shard_map/psum | solution.py:36
  93.4 186.6 %copy-start.15 = (pred[4,300]{1,0:T(4,128)(4,1)}, pred[4,300]{1,0:T(4,128)(4,1)S(1)}, u32[]{:S(2)}) copy-start(pred[4,300]{1,0:T(4,128)(4,1)S(1)} %iota_compare_fusion) | copy-start | bytes 3604
  304.6 14.3 copy-start.11
  304.6 14.3 copy-start.10
  318.9 405.2 %all-reduce.11.cloned.1.call-start = ((), (), s32[]{:S(2)}) async-start(), calls=%async_computation.2 | async-start | bytes 18874368 | tf_op jit(solution)/shard_map/psum | solution.py:40
  488.8 11.8 copy-start.1
  499.9 11.3 slice-start.3
  500.6 10.6 slice-start.4
  500.6 10.6 slice-start.5
  534.8 19.4 %copy-start.7 = (f32[4,1,1152]{2,1,0:T(1,128)S(1)}, f32[4,1,1152]{2,1,0:T(1,128)}, u32[]{:S(2)}) copy-start(f32[4,1,1152]{2,1,0:T(1,128)} %get-tuple-element.17) | copy-start | bytes 55300
  534.8 19.4 %copy-start.5 = (f32[4,6,1152]{2,1,0:T(8,128)S(1)}, f32[4,6,1152]{2,1,0:T(8,128)}, u32[]{:S(2)}) copy-start(f32[4,6,1152]{2,1,0:T(8,128)} %get-tuple-element.15) | copy-start | bytes 331780
  554.1 442.5 %all-reduce.13.cloned.1.call-start = ((), (), s32[]{:S(2)}) async-start(), calls=%async_computation.3 | async-start | bytes 18874368 | tf_op jit(solution)/shard_map/psum | solution.py:31
  768.8 29.7 %copy-start.20 = (bf16[2,4,72,1152]{3,2,1,0:T(8,128)(2,1)S(1)}, bf16[2,4,72,1152]{3,2,1,0:T(8,128)(2,1)}, u32[]{:S(2)}) copy-start(bf16[2,4,72,1152]{3,2,1,0:T(8,128)(2,1)} %param.27) | copy-start | bytes 3981316
  798.6 28.1 %copy-start.12 = (f32[4,1,1152]{2,1,0:T(1,128)S(1)}, f32[4,1,1152]{2,1,0:T(1,128)}, u32[]{:S(2)}) copy-start(f32[4,1,1152]{2,1,0:T(1,128)} %get-tuple-element.14) | copy-start | bytes 55300
  826.6 170.0 %copy-start.4 = (bf16[2,1152,4,72]{1,3,2,0:T(8,128)(2,1)S(1)}, bf16[2,1152,4,72]{1,3,2,0:T(8,128)(2,1)}, u32[]{:S(2)}) copy-start(bf16[2,1152,4,72]{1,3,2,0:T(8,128)(2,1)} %param.28) | copy-start | bytes 3981316
  826.6 394.9 %all-reduce.15.cloned.1.call-start = ((), (), s32[]{:S(2)}) async-start(), calls=%async_computation.4 | async-start | bytes 18874368 | tf_op jit(solution)/shard_map/psum | solution.py:36
  996.6 16.1 %copy-start.16 = (pred[4,300]{1,0:T(4,128)(4,1)S(1)}, pred[4,300]{1,0:T(4,128)(4,1)}, u32[]{:S(2)}) copy-start(pred[4,300]{1,0:T(4,128)(4,1)} %copy-done.15) | copy-start | bytes 3604
  1037.2 14.4 copy-start.9
  1037.2 14.4 copy-start.8
  1051.6 407.8 %all-reduce.17.cloned.1.call-start = ((), (), s32[]{:S(2)}) async-start(), calls=%async_computation.5 | async-start | bytes 18874368 | tf_op jit(solution)/shard_map/psum | solution.py:40
  1250.0 39.5 %copy-start.6 = (f32[4,1,1152]{2,1,0:T(1,128)S(1)}, f32[4,1,1152]{2,1,0:T(1,128)}, u32[]{:S(2)}) copy-start(f32[4,1,1152]{2,1,0:T(1,128)} %get-tuple-element.9) | copy-start | bytes 55300
  1250.0 39.5 %copy-start.14 = (bf16[2,1152]{1,0:T(2,128)(2,1)S(1)}, bf16[2,1152]{1,0:T(2,128)(2,1)}, u32[]{:S(2)}) copy-start(bf16[2,1152]{1,0:T(2,128)(2,1)} %param.33) | copy-start | bytes 13828
  1250.0 39.5 %copy-start.21 = (bf16[32]{0:T(256)(128)(2,1)S(1)}, bf16[32]{0:T(256)(128)(2,1)}, u32[]{:S(2)}) copy-start(bf16[32]{0:T(256)(128)(2,1)} %param.35) | copy-start | bytes 196
  1250.0 39.5 %copy-start.13 = (bf16[8,1152]{1,0:T(8,128)(2,1)S(1)}, bf16[8,1152]{1,0:T(8,128)(2,1)}, u32[]{:S(2)}) copy-start(bf16[8,1152]{1,0:T(8,128)(2,1)} %param.22) | copy-start | bytes 55300
  1289.4 262.0 %all-gather.2.cloned.1.call-start = ((), (), s32[]{:S(2)}) async-start(), calls=%async_computation.6 | async-start | bytes 2621440 | tf_op jit(solution)/shard_map/all_gather | solution.py:85
  1459.3 12.1 copy-start.2
  1459.4 22.4 %slice-start.6 = ((s8[18874368]{0:T(1024)(128)(4,1)}), s8[4194304]{0:T(1024)(128)(4,1)S(1)}, s32[]{:S(2)}) async-start(s8[18874368]{0:T(1024)(128)(4,1)} %bitcast.268), calls=%async_computation.13 | async-start | bytes 8388608
  1459.4 22.4 %slice-start.7 = ((s8[18874368]{0:T(1024)(128)(4,1)}), s8[4194304]{0:T(1024)(128)(4,1)S(1)}, s32[]{:S(2)}) async-start(s8[18874368]{0:T(1024)(128)(4,1)} %bitcast.268), calls=%async_computation.14 | async-start | bytes 8388608
  1459.4 22.4 %slice-start.8 = ((s8[18874368]{0:T(1024)(128)(4,1)}), s8[4194304]{0:T(1024)(128)(4,1)S(1)}, s32[]{:S(2)}) async-start(s8[18874368]{0:T(1024)(128)(4,1)} %bitcast.268), calls=%async_computation.15 | async-start | bytes 8388608
  1471.5 10.3 slice-start.9
  1471.5 10.9 slice-start.10
  1489.9 15.9 %copy-start.17 = (f32[8,2]{0,1:T(2,128)S(1)}, f32[8,2]{0,1:T(2,128)}, u32[]{:S(2)}) copy-start(f32[8,2]{0,1:T(2,128)} %param.24) | copy-start | bytes 196
Sparse Core Ops, SparseCore 0:
  93.4 172.3 all-reduce.6
  319.0 169.7 all-reduce.8
  554.2 169.7 all-reduce.10
  826.7 169.7 all-reduce.12
  1051.7 169.7 all-reduce.14
  1289.5 169.7 all-reduce.16
  1505.9 45.4 all-gather.1
where the time goes:
time: 1570 us; the launch traced here: 1560 us
  waiting for transfers between devices  1060 us (68%)
  matrix products  303 us (19%)
  other arithmetic  168 us (11%)
  local copies, waits for them, and re-layouts  19.9 us (1%)
    psum x2, waiting for transfers between devices, tp_block(): residual = residual + lax.psum(cross_part, 'tp').astype(jnp.float32)  340 us
    psum x2, waiting for transfers between devices, tp_block(): lax.psum(mlp_part, 'tp').astype(jnp.float32)  339 us
    psum x2, waiting for transfers between devices, tp_block(): lax.psum(self_part, 'tp').astype(jnp.float32)  333 us
    reduce_sum x5, other arithmetic, layer_norm(): mean_val = jnp.mean(values, axis=-1, keepdims=True)  68.7 us
    sub x2, matrix products, attention(): attn_prob = jax.nn.softmax(scores, axis=-1).astype(jnp.bfloat16)  59.1 us
    dot_general x2, matrix products, tp_block(): jnp.einsum('rnf,fd->rnd', mlp_hidden, w_fc2, preferred_element_type=jnp.f...  58.7 us
    dot_general x2, matrix products, tp_block(): jnp.einsum('rnhe,hed->rnd', self_o, w_proj, preferred_element_type=jnp.fl...  56.1 us
    sub x2, other arithmetic, attention(): attn_prob = jax.nn.softmax(scores, axis=-1).astype(jnp.bfloat16)  49.2 us
  transfers between devices with their start and end apart: 7, of which 7 were waited for; matrix products, arithmetic and copies ran while one was open for 1% of the time, Pallas kernels for 0%

commit v1 on v0

v1 whole, which is shorter than its diff:
```python
import functools

import jax
import jax.numpy as jnp
from jax import lax
from jax.experimental import pallas as pl
from jax.experimental.pallas import tpu as pltpu
from jax.sharding import PartitionSpec as P


GUIDANCE = 4.5
LN_EPS = 1e-6
HEAD_DIM = 72
VMEM_LIMIT = 62 * 1024 * 1024
LOG2E = 1.4426950408889634
UNITS = 8
NT = (((1,), (1,)), ((), ()))
TN = (((0,), (0,)), ((), ()))


def layer_norm(values):
    mean_val = jnp.mean(values, axis=-1, keepdims=True)
    centered = values - mean_val
    variance = jnp.mean(centered * centered, axis=-1, keepdims=True)
    return centered * lax.rsqrt(variance + LN_EPS)


def dot32(lhs, rhs, dims):
    return lax.dot_general(lhs, rhs, dims, preferred_element_type=jnp.float32)


def unit_copy(unit_refs, scratch, sems, index, offset, rows):
    array, lead = unit_refs[index]
    src = array.at[lead, pl.ds(offset, rows)] if lead is not None else array.at[pl.ds(offset, rows)]
    return pltpu.make_async_copy(src, scratch.at[pl.ds(index * rows, rows)], sems.at[index])


def unit_list(own, partner, rest):
    return [(own, 0), (own, 1), (partner, 0), (partner, 1)] + [(ref, None) for ref in rest]


def start_units(unit_refs, scratch, sems, offset, rows):
    for index in range(UNITS):
        unit_copy(unit_refs, scratch, sems, index, offset, rows).start()


def wait_units(unit_refs, scratch, sems, offset, rows, first=0, last=UNITS):
    for index in range(first, last):
        unit_copy(unit_refs, scratch, sems, index, offset, rows).wait()


def call(kernel, grid, in_specs, out_specs, out_shape, scratch, flops, nbytes):
    return pl.pallas_call(
        kernel, grid=grid, in_specs=in_specs, out_specs=out_specs, out_shape=out_shape, scratch_shapes=scratch,
        compiler_params=pltpu.CompilerParams(dimension_semantics=('arbitrary',), vmem_limit_bytes=VMEM_LIMIT),
        cost_estimate=pl.CostEstimate(flops=int(flops), bytes_accessed=int(nbytes), transcendentals=0))


ANY = pl.BlockSpec(memory_space=pl.ANY)


def whole(shape):
    return pl.BlockSpec(shape, lambda *_: (0,) * len(shape))


def qkv_kernel(x_ref, mod_ref, own, partner, y, x, ys, xs, out_ref, a_buf, w_buf, sems):
    units = unit_list(own, partner, [y, x, ys, xs])
    rows = own.shape[1]
    step = pl.program_id(0)

    @pl.when(step == 0)
    def _():
        start_units(units, w_buf, sems, 0, rows)

        @pl.loop(0, x_ref.shape[0] // 128)
        def _(chunk):
            sl = pl.ds(pl.multiple_of(chunk * 128, 128), 128)
            vals = layer_norm(x_ref[sl, :].astype(jnp.float32))
            a_buf[sl, :] = (vals * (1.0 + mod_ref[1:2, :]) + mod_ref[0:1, :]).astype(jnp.bfloat16)

    for index in range(UNITS):
        @pl.when(step == index)
        def _():
            unit_copy(units, w_buf, sems, index, 0, rows).wait()
    res = dot32(w_buf[pl.ds(pl.multiple_of(step * rows, 16), rows), :], a_buf[...], NT)
    for j in range(rows // HEAD_DIM):
        out_ref[j] = res[j * HEAD_DIM:(j + 1) * HEAD_DIM].astype(jnp.bfloat16)


def qkv_call(x, mod, units):
    tokens, dim = x.shape
    rows = units[0].shape[1]
    per = rows // HEAD_DIM
    return call(
        qkv_kernel, (UNITS,), [whole((tokens, dim)), whole(mod.shape)] + [ANY] * 6,
        pl.BlockSpec((per, HEAD_DIM, tokens), lambda i: (i, 0, 0)),
        jax.ShapeDtypeStruct((UNITS * per, HEAD_DIM, tokens), jnp.bfloat16),
        [pltpu.VMEM((tokens, dim), jnp.bfloat16), pltpu.VMEM((UNITS * rows, dim), jnp.bfloat16), pltpu.SemaphoreType.DMA((UNITS,))],
        2 * tokens * dim * rows * UNITS, 4 * tokens * dim + 4 * rows * UNITS * dim)(x, mod, *units)


def softmax_out(scores, v_t, scale):
    top = jnp.max(scores, axis=0, keepdims=True)
    prob = jnp.exp2((scores - top) * scale)
    total = jnp.sum(prob, axis=0, keepdims=True)
    return dot32(v_t, prob.astype(jnp.bfloat16), (((1,), (0,)), ((), ()))) * (1.0 / total)


def self_attn_kernel(qkv_ref, out_ref, *, chunk):
    scale = HEAD_DIM ** -0.5 * LOG2E
    tokens = qkv_ref.shape[2]
    keys = [qkv_ref[3 * h + 1].astype(jnp.float32).T.astype(jnp.bfloat16) for h in range(2)]
    vals = [qkv_ref[3 * h + 2] for h in range(2)]
    for start in range(0, tokens, chunk):
        sl = slice(start, start + chunk)
        scores = [dot32(keys[h], qkv_ref[3 * h, :, sl], (((1,), (0,)), ((), ()))) for h in range(2)]
        outs = [softmax_out(scores[h], vals[h], scale) for h in range(2)]
        out_ref[:, sl] = jnp.concatenate(outs, axis=0).astype(jnp.bfloat16)


def self_attn_call(qkv):
    n_vecs, _, tokens = qkv.shape
    heads = n_vecs // 3
    return call(
        functools.partial(self_attn_kernel, chunk=256), (heads // 2,),
        [pl.BlockSpec((6, HEAD_DIM, tokens), lambda i: (i, 0, 0))],
        pl.BlockSpec((2 * HEAD_DIM, tokens), lambda i: (i, 0)),
        jax.ShapeDtypeStruct((heads * HEAD_DIM, tokens), jnp.bfloat16), [],
        heads * 4 * tokens * tokens * 256, n_vecs * HEAD_DIM * tokens * 4)(qkv)


def proj_kernel(o_ref, x_ref, mod_ref, own, partner, y, x, ys, xs, x_out, q_out, p_buf, q_buf, p_sems, q_sems):
    units = unit_list(own, partner, [y, x, ys, xs])
    rows = 2 * HEAD_DIM

    @pl.when(pl.program_id(0) == 0)
    def _():
        start_units(units, p_buf, p_sems, 0, rows)
        start_units(units, q_buf, q_sems, rows, rows)
        wait_units(units, p_buf, p_sems, 0, rows)

    part = dot32(o_ref[...], p_buf[...], TN).astype(jnp.bfloat16).astype(jnp.float32)
    resid = x_ref[...].astype(jnp.float32) + mod_ref[2:3, :] * part
    x_out[...] = resid

    @pl.when(pl.program_id(0) == 0)
    def _():
        wait_units(units, q_buf, q_sems, rows, rows)

    q_t = dot32(q_buf[...], resid.astype(jnp.bfloat16), NT)
    for h in range(q_out.shape[0]):
        q_out[h] = q_t[h * HEAD_DIM:(h + 1) * HEAD_DIM].astype(jnp.bfloat16)


def proj_call(o_t, x, mod, units, chunk=512):
    tokens, dim = x.shape
    heads = UNITS * 2
    return call(
        proj_kernel, (tokens // chunk,),
        [pl.BlockSpec((dim, chunk), lambda i: (0, i)), pl.BlockSpec((chunk, dim), lambda i: (i, 0)), whole(mod.shape)] + [ANY] * 6,
        [pl.BlockSpec((chunk, dim), lambda i: (i, 0)), pl.BlockSpec((heads, HEAD_DIM, chunk), lambda i: (0, 0, i))],
        [jax.ShapeDtypeStruct((tokens, dim), jnp.float32), jax.ShapeDtypeStruct((heads, HEAD_DIM, tokens), jnp.bfloat16)],
        [pltpu.VMEM((dim, dim), jnp.bfloat16)] * 2 + [pltpu.SemaphoreType.DMA((UNITS,))] * 2,
        4 * tokens * dim * dim, 12 * tokens * dim)(o_t, x, mod, *units)


def ckv_kernel(cap_ref, own, partner, y, x, ys, xs, out_ref, w_buf, sems):
    units = unit_list(own, partner, [y, x, ys, xs])
    rows = 4 * HEAD_DIM
    step = pl.program_id(0)

    @pl.when(step == 0)
    def _():
        start_units(units, w_buf, sems, 6 * HEAD_DIM, rows)

    for index in range(UNITS):
        @pl.when(step == index)
        def _():
            unit_copy(units, w_buf, sems, index, 6 * HEAD_DIM, rows).wait()
    res = dot32(w_buf[pl.ds(pl.multiple_of(step * rows, 16), rows), :], cap_ref[...], NT)
    for j in range(4):
        out_ref[j] = res[j * HEAD_DIM:(j + 1) * HEAD_DIM].astype(jnp.bfloat16)


def ckv_call(cap, units):
    text, dim = cap.shape
    return call(
        ckv_kernel, (UNITS,), [whole((text, dim))] + [ANY] * 6,
        pl.BlockSpec((4, HEAD_DIM, text), lambda i: (i, 0, 0)),
        jax.ShapeDtypeStruct((4 * UNITS, HEAD_DIM, text), jnp.bfloat16),
        [pltpu.VMEM((UNITS * 4 * HEAD_DIM, dim), jnp.bfloat16), pltpu.SemaphoreType.DMA((UNITS,))],
        2 * text * dim * 2 * dim, 4 * dim * dim)(cap, *units)


def cross_attn_kernel(len_ref, q_ref, kv_ref, out_ref, *, chunk, text):
    scale = HEAD_DIM ** -0.5 * LOG2E
    tokens = q_ref.shape[2]
    keys = [kv_ref[2 * h].astype(jnp.float32).T[:text].astype(jnp.bfloat16) for h in range(2)]
    vals = [kv_ref[2 * h + 1][:, :text] for h in range(2)]
    live = lax.broadcasted_iota(jnp.int32, (text, chunk), 0) < len_ref[0]
    for start in range(0, tokens, chunk):
        sl = slice(start, start + chunk)
        scores = [dot32(keys[h], q_ref[h, :, sl], (((1,), (0,)), ((), ()))) for h in range(2)]
        outs = [softmax_out(jnp.where(live, scores[h], -1e30), vals[h], scale) for h in range(2)]
        out_ref[:, sl] = jnp.concatenate(outs, axis=0).astype(jnp.bfloat16)


def cross_attn_call(cap_len, q_t, kv_t, text):
    heads, _, tokens = q_t.shape
    return call(
        functools.partial(cross_attn_kernel, chunk=256, text=text), (heads // 2,),
        [pl.BlockSpec(memory_space=pltpu.SMEM), pl.BlockSpec((2, HEAD_DIM, tokens), lambda i: (i, 0, 0)),
         pl.BlockSpec((4, HEAD_DIM, kv_t.shape[2]), lambda i: (i, 0, 0))],
        pl.BlockSpec((2 * HEAD_DIM, tokens), lambda i: (i, 0)),
        jax.ShapeDtypeStruct((heads * HEAD_DIM, tokens), jnp.bfloat16), [],
        heads * 4 * tokens * text * 256, heads * HEAD_DIM * tokens * 4)(cap_len, q_t, kv_t)


def fc1_kernel(o_ref, x_ref, mod_ref, own, partner, y, x, ys, xs, own1, partner1, y1, x1, ys1, xs1, x_out, u_out, p_buf, w_buf, p_sems, w_sems):
    units = unit_list(own, partner, [y, x, ys, xs])
    fc_units = unit_list(own1, partner1, [y1, x1, ys1, xs1])
    rows = 2 * HEAD_DIM
    fc_rows = own1.shape[1]
    first = pl.program_id(0) == 0

    @pl.when(first)
    def _():
        start_units(units, p_buf, p_sems, 2 * rows, rows)
        start_units(fc_units, w_buf, w_sems, 0, fc_rows)
        wait_units(units, p_buf, p_sems, 2 * rows, rows)

    part = dot32(o_ref[...], p_buf[...], TN).astype(jnp.bfloat16).astype(jnp.float32)
    resid = x_ref[...] + part
    x_out[...] = resid
    mlp_in = (layer_norm(resid) * (1.0 + mod_ref[4:5, :]) + mod_ref[3:4, :]).astype(jnp.bfloat16)
    for pair in range(UNITS // 2):
        @pl.when(first)
        def _():
            wait_units(fc_units, w_buf, w_sems, 0, fc_rows, 2 * pair, 2 * pair + 2)

        cols = slice(2 * pair * fc_rows, 2 * (pair + 1) * fc_rows)
        u_out[:, cols] = jax.nn.gelu(dot32(mlp_in, w_buf[cols, :], NT), approximate=True).astype(jnp.bfloat16)


def fc1_call(o_t, x, mod, units, fc_units, chunk=512):
    tokens, dim = x.shape
    hidden = UNITS * fc_units[0].shape[1]
    return call(
        fc1_kernel, (tokens // chunk,),
        [pl.BlockSpec((dim, chunk), lambda i: (0, i)), pl.BlockSpec((chunk, dim), lambda i: (i, 0)), whole(mod.shape)] + [ANY] * 12,
        [pl.BlockSpec((chunk, dim), lambda i: (i, 0)), pl.BlockSpec((chunk, hidden), lambda i: (i, 0))],
        [jax.ShapeDtypeStruct((tokens, dim), jnp.float32), jax.ShapeDtypeStruct((tokens, hidden), jnp.bfloat16)],
        [pltpu.VMEM((dim, dim), jnp.bfloat16), pltpu.VMEM((hidden, dim), jnp.bfloat16)] + [pltpu.SemaphoreType.DMA((UNITS,))] * 2,
        2 * tokens * dim * (dim + hidden), 2 * tokens * hidden + 8 * tokens * dim)(o_t, x, mod, *units, *fc_units)


def fc2_kernel(u_ref, x_ref, mod_ref, own, partner, y, x, ys, xs, *rest):
    units = unit_list(own, partner, [y, x, ys, xs])
    *head, out_ref, w_buf, sems = rest
    rows = own.shape[1]
    half = UNITS // 2 * rows
    first = pl.program_id(0) == 0

    @pl.when(first)
    def _():
        start_units(units, w_buf, sems, 0, rows)
        wait_units(units, w_buf, sems, 0, rows, 0, UNITS // 2)

    total = dot32(u_ref[:, :half], w_buf[:half, :], (((1,), (0,)), ((), ())))

    @pl.when(first)
    def _():
        wait_units(units, w_buf, sems, 0, rows, UNITS // 2, UNITS)

    total = total + dot32(u_ref[:, half:], w_buf[half:, :], (((1,), (0,)), ((), ())))
    resid = x_ref[...] + mod_ref[5:6, :] * total.astype(jnp.bfloat16).astype(jnp.float32)
    if head:
        shift_scale, w_eps, b_eps = head
        final_in = (layer_norm(resid) * (1.0 + shift_scale[1:2, :]) + shift_scale[0:1, :]).astype(jnp.bfloat16)
        out_ref[...] = dot32(w_eps[...], final_in, NT) + b_eps[:, 0:1]
    else:
        out_ref[...] = resid


def fc2_call(u, x, mod, units, head=(), chunk=512):
    tokens, dim = x.shape
    hidden = u.shape[1]
    out_spec = pl.BlockSpec((16, chunk), lambda i: (0, i)) if head else pl.BlockSpec((chunk, dim), lambda i: (i, 0))
    return call(
        fc2_kernel, (tokens // chunk,),
        [pl.BlockSpec((chunk, hidden), lambda i: (i, 0)), pl.BlockSpec((chunk, dim), lambda i: (i, 0)), whole(mod.shape)] + [ANY] * 6 + [whole(h.shape) for h in head],
        out_spec, jax.ShapeDtypeStruct((16, tokens) if head else (tokens, dim), jnp.float32),
        [pltpu.VMEM((hidden, dim), jnp.bfloat16), pltpu.SemaphoreType.DMA((UNITS,))],
        2 * tokens * dim * hidden, 2 * tokens * hidden + 8 * tokens * dim)(u, x, mod, *units, *head)


def local_units(w_qkv, w_proj, w_cq, w_ckv, w_cproj, w_fc1, w_fc2):
    dim = w_qkv.shape[0]

    def halves(weight):
        return weight.reshape(2, -1, dim)

    qkv = halves(w_qkv.transpose(2, 1, 3, 0))
    misc = jnp.concatenate([halves(w_proj), halves(w_cq.transpose(1, 2, 0)), halves(w_cproj), halves(w_ckv.transpose(2, 1, 3, 0))], axis=1)
    return [qkv, misc, halves(w_fc1.T), halves(w_fc2)]


SWAP = [(i, i ^ 1) for i in range(4)]


class Group:
    def __init__(self, own):
        self.own = own
        half = lax.dynamic_index_in_dim(own, lax.axis_index('dp'), 0, keepdims=False)
        self.over_y = lax.ppermute(half, 'tp', [(i, i ^ 2) for i in range(4)])
        self.partner = lax.ppermute(own, 'tp', SWAP)

    def relay(self, tok):
        self.over_y, tok = lax.optimization_barrier((self.over_y, tok))
        self.over_x = lax.ppermute(self.over_y, 'dp', [(0, 1), (1, 0)])
        self.y_swap = lax.ppermute(self.over_y, 'tp', SWAP)
        return tok

    def finish(self, tok):
        self.over_x, tok = lax.optimization_barrier((self.over_x, tok))
        self.x_swap = lax.ppermute(self.over_x, 'tp', SWAP)
        return tok

    def units(self):
        return [self.own, self.partner, self.over_y, self.over_x, self.y_swap, self.x_swap]


def transformer(x, cap, cap_len, mods, groups, head, text):
    n_layers = len(groups)
    x = groups[0][0].relay(x)
    x = groups[0][0].finish(x)
    for layer in range(n_layers):
        qkv_g, misc_g, fc1_g, fc2_g = groups[layer]
        mod = mods[layer]
        following = groups[layer + 1][0] if layer + 1 < n_layers else None
        qkv = qkv_call(x, mod, qkv_g.units())
        qkv = misc_g.relay(qkv)
        o_t = self_attn_call(qkv)
        o_t = misc_g.finish(fc1_g.relay(o_t))
        kv_t = ckv_call(cap, misc_g.units())
        x1, q_t = proj_call(o_t, x, mod, misc_g.units())
        q_t = fc2_g.relay(q_t) if layer else q_t
        oc_t = cross_attn_call(cap_len, q_t, kv_t, text)
        oc_t = fc1_g.finish(oc_t)
        oc_t = oc_t if layer else fc2_g.relay(oc_t)
        x2, hid = fc1_call(oc_t, x1, mod, misc_g.units(), fc1_g.units())
        hid = fc2_g.finish(following.relay(hid) if following else hid)
        if following:
            x = fc2_call(hid, x2, mod, fc2_g.units())
            x = following.finish(x)
    return fc2_call(hid, x2, mod, fc2_g.units(), head)


def ddim_update(guided, x_t, alpha_bar):
    abar_t = alpha_bar[:, 0][:, None, None, None]
    abar_prev = alpha_bar[:, 1][:, None, None, None]
    x_zero = (x_t - jnp.sqrt(1.0 - abar_t) * guided) / jnp.sqrt(abar_t)
    return jnp.sqrt(abar_prev) * x_zero + jnp.sqrt(1.0 - abar_prev) * guided


def solution(mesh):
    row_spec = P(('dp', 'cfg'))
    part_spec = P('dp')
    in_specs = (row_spec, row_spec, row_spec, part_spec, part_spec, part_spec, part_spec, P(),
                P(None, None, None, 'tp'), P(None, 'tp'), P(None, None, 'tp'), P(None, None, None, 'tp'),
                P(None, 'tp'), P(None, None, 'tp'), P(None, 'tp'), P(), P(), P())

    def local_step(hidden, caption, cap_len, t_block, t_embed, x_t, alpha_bar, mod_table, w_qkv, w_proj, w_cq, w_ckv, w_cproj, w_fc1, w_fc2, final_table, w_out, b_out):
        dim = hidden.shape[2]
        n_images = t_block.shape[0]
        tp, cfg = lax.axis_index('tp'), lax.axis_index('cfg')
        image = (cfg * hidden.shape[0] + tp) % n_images
        layers = []
        for layer in range(mod_table.shape[0]):
            own = local_units(w_qkv[layer], w_proj[layer], w_cq[layer], w_ckv[layer], w_cproj[layer], w_fc1[layer], w_fc2[layer])
            layers.append([Group(group) for group in own])
        x = lax.dynamic_index_in_dim(hidden, tp, 0, keepdims=False)
        n_text = caption.shape[1]
        text = -(-n_text // 16) * 16
        cap = jnp.pad(lax.dynamic_index_in_dim(caption, tp, 0, keepdims=False), ((0, -(-n_text // 128) * 128 - n_text), (0, 0)))
        row_len = lax.dynamic_slice_in_dim(cap_len, tp, 1, 0)
        t_mods = lax.dynamic_index_in_dim(t_block, image, 0, keepdims=False).astype(jnp.float32).reshape(6, dim)
        emb = lax.dynamic_index_in_dim(t_embed, image, 0, keepdims=False).astype(jnp.float32)
        mods = [mod_table[layer].astype(jnp.float32) + t_mods for layer in range(mod_table.shape[0])]
        w_eps = w_out.reshape(dim, 4, 8)[:, :, :4].reshape(dim, 16).T
        b_eps = jnp.broadcast_to(b_out.astype(jnp.float32).reshape(4, 8)[:, :4].reshape(16, 1), (16, 128))
        head = (final_table.astype(jnp.float32) + emb[None, :], w_eps, b_eps)
        eps = transformer(x, cap, row_len, mods, layers, head, text)
        other = lax.ppermute(eps, 'cfg', [(i, (i + 2) % 4) for i in range(4)])
        is_cond = cfg < 2
        eps_cond = jnp.where(is_cond, eps, other)
        eps_uncond = jnp.where(is_cond, other, eps)
        guided = eps_uncond + GUIDANCE * (eps_cond - eps_uncond)
        mine = lax.all_gather(guided, 'tp', axis=0)
        theirs = lax.ppermute(mine, 'cfg', [(i, i ^ 1) for i in range(4)])
        even = cfg % 2 == 0
        guided = jnp.concatenate([jnp.where(even, mine, theirs), jnp.where(even, theirs, mine)], axis=0)
        side = x_t.shape[1] // 2
        guided = guided.reshape(n_images, 2, 2, 4, side, side).transpose(0, 4, 1, 5, 2, 3).reshape(x_t.shape)
        return ddim_update(guided, x_t, alpha_bar)

    return jax.shard_map(local_step, mesh=mesh, in_specs=in_specs, out_specs=part_spec, check_vma=False)
```

time: 1570 us -> 485 us (0.31)
  waiting for transfers between devices: 1060 us -> 78.3 us
  matrix products: 303 us -> 0 us
  Pallas kernels: 0 us -> 281 us
  other arithmetic: 168 us -> 7.94 us
  local copies, waits for them, and re-layouts: 19.9 us -> 77 us
  starting transfers between devices: 0.25 us -> 25.4 us
    psum x6 -> x0, waiting for transfers between devices: 1010 us -> none  [the longest x2 340 us: tp_block(): residual = residual + lax.psum(cross_part, 'tp').astype(jnp.float32)]
    pallas_call x0 -> x14, Pallas kernels: none -> 281 us  [the longest x2 66 us: fc1_call(): call(fc1_kernel, (tokens // chunk,), [pl.BlockSpec((dim, chunk), lambda i...]
    dot_general x14 -> x0, matrix products: 244 us -> none  [the longest x2 58.7 us: tp_block(): jnp.einsum('rnf,fd->rnd', mlp_hidden, w_fc2, preferred_element_type=jnp.f...]
    reduce_sum x10 -> x0, other arithmetic: 113 us -> none  [the longest x5 68.7 us: layer_norm(): mean_val = jnp.mean(values, axis=-1, keepdims=True)]
    ppermute x0 -> x42, waiting for transfers between devices: none -> 78.3 us  [the longest x8 42.9 us: __init__(): self.over_y = lax.ppermute(half, 'tp', [(i, i ^ 2) for i in range(4)])]
    sub x2 -> x0, matrix products: 59.1 us -> none  [attention(): attn_prob = jax.nn.softmax(scores, axis=-1).astype(jnp.bfloat16)]
    sub x2 -> x0, other arithmetic: 49.2 us -> none  [attention(): attn_prob = jax.nn.softmax(scores, axis=-1).astype(jnp.bfloat16)]
    all_gather x1 -> x0, waiting for transfers between devices: 45.6 us -> none  [local_step(): eps_all = lax.all_gather(eps_local, 'cfg', axis=0, tiled=True)]
  transfers between devices with their start and end apart: 7 -> 42, of which waited for: 7 -> 12; matrix products, arithmetic and copies ran while one was open for 1% -> 12% of each run, Pallas kernels for 0% -> 54%
where the time goes in v1:
time: 485 us; the launch traced here: 476 us
  Pallas kernels  281 us (58%)
  waiting for transfers between devices  78.3 us (16%)
  local copies, waits for them, and re-layouts  77 us (16%)
  starting transfers between devices  25.4 us (5%)
  other arithmetic  7.94 us (2%)
  blocking collectives  5.78 us (1%)
    pallas_call x2, Pallas kernels, fc1_call(): call(fc1_kernel, (tokens // chunk,), [pl.BlockSpec((dim, chunk), lambda i...  66 us
    pallas_call x2, Pallas kernels, self_attn_call(): call(functools.partial(self_attn_kernel, chunk=256), (heads // 2,), [pl.B...  59 us
    pallas_call x2, Pallas kernels, fc2_call(): call(fc2_kernel, (tokens // chunk,), [pl.BlockSpec((chunk, hidden), lambd...  48 us
    ppermute x8, waiting for transfers between devices, __init__(): self.over_y = lax.ppermute(half, 'tp', [(i, i ^ 2) for i in range(4)])  42.9 us
    pallas_call x2, Pallas kernels, qkv_call(): call(qkv_kernel, (UNITS,), [whole((tokens, dim)), whole(mod.shape)] + [AN...  32.4 us
    pallas_call x2, Pallas kernels, cross_attn_call(): call(functools.partial(cross_attn_kernel, chunk=256, text=text), (heads /...  31.8 us
    pallas_call x2, Pallas kernels, proj_call(): call(proj_kernel, (tokens // chunk,), [pl.BlockSpec((dim, chunk), lambda...  28.3 us
    ppermute x8, waiting for transfers between devices, relay(): self.over_x = lax.ppermute(self.over_y, 'dp', [(0, 1), (1, 0)])  20.9 us
  transfers between devices with their start and end apart: 42, of which 12 were waited for; matrix products, arithmetic and copies ran while one was open for 12% of the time, Pallas kernels for 54%

profile of v1, /device:TPU:0, one launch (start us, length us, event | category | flops | bytes accessed | tf_op | source)
XLA Modules:
  0.0 476.2 jit_solution(17241807536477201904)
XLA Ops:
  0.0 3.8 slice_bitcast_fusion.2
  5.7 2.2 dynamic-slice_bitcast_fusion.7
  8.0 2.6 collective-permute-start.6
  16.1 1.9 pad_maximum_fusion.1.own
  18.1 2.7 dynamic-slice_bitcast_fusion.1
  21.1 3.3 dynamic-slice_bitcast_fusion.x_ref
  24.4 9.3 %collective-permute-done.6.y = bf16[432,1152]{1,0:T(8,128)(2,1)} collective-permute-done((bf16[432,1152]{1,0:T(8,128)(2,1)}, bf16[432,1152]{1,0:T(8,128)(2,1)}, u32[]{:S(2)}, u32[]{:S(2)}) %collective-permute-start.6) | collective-permute-done | bytes 995360 | tf_op jit(solution)/shard_map/ppermute | solution.py:315
  33.7 2.0 collective-permute-start.7
  35.7 4.5 slice_bitcast_fusion
  40.2 3.3 copy.53
  43.5 14.1 %collective-permute-done.7.x = bf16[432,1152]{1,0:T(8,128)(2,1)} collective-permute-done((bf16[432,1152]{1,0:T(8,128)(2,1)}, bf16[432,1152]{1,0:T(8,128)(2,1)}, u32[]{:S(2)}, u32[]{:S(2)}) %collective-permute-start.7) | collective-permute-done | bytes 995360 | tf_op jit(solution)/shard_map/ppermute | solution.py:320
  57.6 2.5 dynamic-slice_bitcast_fusion.4
  64.8 15.9 %shard_map.172.qkv_ref = bf16[48,72,1024]{2,1,0:T(8,128)(2,1)} custom-call(bf16[1024,1152]{1,0:T(8,128)(2,1)} %dynamic-slice_bitcast_fusion.x_ref, f32[6,1152]{1,0:T(8,128)} %get-tuple-element.102.mod_ref, bf16[2,432,1152]{2,1,0:T(8,128)(2,1)} %bitcast.34.own, bf16[2,432,1152]{2,1,0:T(8,128)(2,1)} %collective-permute-done.8.partner, ...), custom_call_target="tpu_custom_call" | custom-call | flops 8153726976 | bytes 20643840 | tf_op jit(solution)/shard_map/pallas_call | solution.py:94
  80.6 1.6 collective-permute-start.12
  82.2 3.2 constant_dynamic-slice_fusion
  87.1 29.5 %shard_map.173.o_ref = bf16[1152,1024]{1,0:T(8,128)(2,1)} custom-call(bf16[48,72,1024]{2,1,0:T(8,128)(2,1)} %shard_map.172.qkv_ref), custom_call_target="tpu_custom_call" | custom-call | flops 17179869184 | bytes 14155776 | tf_op jit(solution)/shard_map/pallas_call | solution.py:124
  116.6 2.3 collective-permute-done.12.x
  118.9 5.1 %fusion.3 = (bf16[1,1152,1152]{2,1,0:T(8,128)(2,1)S(1)}, bf16[1,1152,1152]{2,1,0:T(8,128)(2,1)}) fusion(bf16[2,1152,1152]{2,1,0:T(8,128)(2,1)} %param.32), kind=kLoop, calls=%fused_computation.39 | loop fusion | bytes 10616832 | tf_op jit(solution)/shard_map/slice | solution.py:380
  127.3 7.9 %shard_map.175.kv_ref = bf16[32,72,384]{2,1,0:T(8,128)(2,1)} custom-call(bf16[384,1152]{1,0:T(8,128)(2,1)} %pad.4.cap_ref, bf16[2,720,1152]{2,1,0:T(8,128)(2,1)} %pad_maximum_fusion.1.own, bf16[2,720,1152]{2,1,0:T(8,128)(2,1)} %collective-permute-done.13.partner, bf16[720,1152]{1,0:T(8,128)(2,1)} %collective-permute-done.5.y, bf16[720,1152]{1,0:T(8,128)(2,1)} %copy-done.10, ...), custom_call_target="tpu_custom_call" | custom-call | flops 2038431744 | bytes 5308416 | tf_op jit(solution)/shard_map/pallas_call | solution.py:187
  135.2 14.0 %shard_map.174 = (f32[1024,1152]{1,0:T(8,128)}, bf16[16,72,1024]{2,1,0:T(8,128)(2,1)}) custom-call(bf16[1152,1024]{1,0:T(8,128)(2,1)} %shard_map.173.o_ref, bf16[1024,1152]{1,0:T(8,128)(2,1)} %dynamic-slice_bitcast_fusion.x_ref, f32[6,1152]{1,0:T(8,128)} %get-tuple-element.102.mod_ref, bf16[2,720,1152]{2,1,0:T(8,128)(2,1)} %pad_maximum_fusion.1.own, ...), custom_call_target="tpu_custom_call" | custom-call | flops 5435817984 | bytes 14155776 | tf_op jit(solution)/shard_map/pallas_call | solution.py:158
  149.2 16.0 %shard_map.176.o_ref = bf16[1152,1024]{1,0:T(8,128)(2,1)} custom-call(s32[1]{0:T(128)} %dynamic_slice.55.len_ref, bf16[16,72,1024]{2,1,0:T(8,128)(2,1)} %get-tuple-element.55.q_ref, bf16[32,72,384]{2,1,0:T(8,128)(2,1)} %shard_map.175.kv_ref), custom_call_target="tpu_custom_call" | custom-call | flops 5100273664 | bytes 4718592 | tf_op jit(solution)/shard_map/pallas_call | solution.py:210
  165.9 1.5 collective-permute-start.20
  168.4 1.5 collective-permute-start.2
  171.0 33.0 %shard_map.177 = (f32[1024,1152]{1,0:T(8,128)}, bf16[1024,4608]{1,0:T(8,128)(2,1)}) custom-call(bf16[1152,1024]{1,0:T(8,128)(2,1)} %shard_map.176.o_ref, f32[1024,1152]{1,0:T(8,128)} %get-tuple-element.58.x_ref, f32[6,1152]{1,0:T(8,128)} %get-tuple-element.102.mod_ref, bf16[2,720,1152]{2,1,0:T(8,128)(2,1)} %pad_maximum_fusion.1.own, ...), custom_call_target="tpu_custom_call" | custom-call | flops 13589544960 | bytes 18874368 | tf_op jit(solution)/shard_map/pallas_call | solution.py:248
  205.6 1.9 pad_maximum_fusion.own
  208.2 23.3 %shard_map.178.x_ref = f32[1024,1152]{1,0:T(8,128)} custom-call(bf16[1024,4608]{1,0:T(8,128)(2,1)} %get-tuple-element.64.u_ref, f32[1024,1152]{1,0:T(8,128)} %get-tuple-element.65.x_ref, f32[6,1152]{1,0:T(8,128)} %get-tuple-element.102.mod_ref, bf16[2,576,1152]{2,1,0:T(8,128)(2,1)} %bitcast.99, bf16[2,576,1152]{2,1,0:T(8,128)(2,1)} %collective-permute-done.21.partner, ...), custom_call_target="tpu_custom_call" | custom-call | flops 10871635968 | bytes 18874368 | tf_op jit(solution)/shard_map/pallas_call | solution.py:289
  232.2 2.9 dynamic-slice_bitcast_fusion.2
  236.0 3.3 copy.59
  239.3 16.5 %shard_map.179.qkv_ref = bf16[48,72,1024]{2,1,0:T(8,128)(2,1)} custom-call(f32[1024,1152]{1,0:T(8,128)} %shard_map.178.x_ref, f32[6,1152]{1,0:T(8,128)} %get-tuple-element.101.mod_ref, bf16[2,432,1152]{2,1,0:T(8,128)(2,1)} %bitcast.104, bf16[2,432,1152]{2,1,0:T(8,128)(2,1)} %collective-permute-done.24.partner, bf16[432,1152]{1,0:T(8,128)(2,1)} %collective-permute-done.2.y, ...), custom_call_target="tpu_custom_call" | custom-call | flops 8153726976 | bytes 20643840 | tf_op jit(solution)/shard_map/pallas_call | solution.py:94
  255.8 18.2 %collective-permute-done.1.y = bf16[720,1152]{1,0:T(8,128)(2,1)} collective-permute-done((bf16[720,1152]{1,0:T(8,128)(2,1)}, bf16[720,1152]{1,0:T(8,128)(2,1)}, u32[]{:S(2)}, u32[]{:S(2)}) %collective-permute-start.1) | collective-permute-done | bytes 1658912 | tf_op jit(solution)/shard_map/ppermute | solution.py:315
  275.0 2.5 dynamic-slice_bitcast_fusion.3
  278.1 29.5 %shard_map.180.o_ref = bf16[1152,1024]{1,0:T(8,128)(2,1)} custom-call(bf16[48,72,1024]{2,1,0:T(8,128)(2,1)} %shard_map.179.qkv_ref), custom_call_target="tpu_custom_call" | custom-call | flops 17179869184 | bytes 14155776 | tf_op jit(solution)/shard_map/pallas_call | solution.py:124
  308.0 3.9 collective-permute-done.27.x
  311.9 3.1 dynamic-slice_bitcast_fusion.6
  316.9 14.4 %shard_map.181 = (f32[1024,1152]{1,0:T(8,128)}, bf16[16,72,1024]{2,1,0:T(8,128)(2,1)}) custom-call(bf16[1152,1024]{1,0:T(8,128)(2,1)} %shard_map.180.o_ref, f32[1024,1152]{1,0:T(8,128)} %shard_map.178.x_ref, f32[6,1152]{1,0:T(8,128)} %get-tuple-element.101.mod_ref, bf16[2,720,1152]{2,1,0:T(8,128)(2,1)} %pad_maximum_fusion.own, ...), custom_call_target="tpu_custom_call" | custom-call | flops 5435817984 | bytes 14155776 | tf_op jit(solution)/shard_map/pallas_call | solution.py:158
  331.3 15.0 %collective-permute-done.y = bf16[576,1152]{1,0:T(8,128)(2,1)} collective-permute-done((bf16[576,1152]{1,0:T(8,128)(2,1)}, bf16[576,1152]{1,0:T(8,128)(2,1)}, u32[]{:S(2)}, u32[]{:S(2)}) %collective-permute-start) | collective-permute-done | bytes 1327136 | tf_op jit(solution)/shard_map/ppermute | solution.py:315
  346.3 7.8 %shard_map.182.kv_ref = bf16[32,72,384]{2,1,0:T(8,128)(2,1)} custom-call(bf16[384,1152]{1,0:T(8,128)(2,1)} %pad.4.cap_ref, bf16[2,720,1152]{2,1,0:T(8,128)(2,1)} %pad_maximum_fusion.own, bf16[2,720,1152]{2,1,0:T(8,128)(2,1)} %collective-permute-done.29.partner, bf16[720,1152]{1,0:T(8,128)(2,1)} %collective-permute-done.1.y, bf16[720,1152]{1,0:T(8,128)(2,1)} %copy-done.2, ...), custom_call_target="tpu_custom_call" | custom-call | flops 2038431744 | bytes 5308416 | tf_op jit(solution)/shard_map/pallas_call | solution.py:187
  354.1 15.8 %shard_map.183.o_ref = bf16[1152,1024]{1,0:T(8,128)(2,1)} custom-call(s32[1]{0:T(128)} %dynamic_slice.55.len_ref, bf16[16,72,1024]{2,1,0:T(8,128)(2,1)} %get-tuple-element.77.q_ref, bf16[32,72,384]{2,1,0:T(8,128)(2,1)} %shard_map.182.kv_ref), custom_call_target="tpu_custom_call" | custom-call | flops 5100273664 | bytes 4718592 | tf_op jit(solution)/shard_map/pallas_call | solution.py:210
  371.3 1.8 collective-permute-done.36.xs1
  374.3 33.0 %shard_map.184 = (f32[1024,1152]{1,0:T(8,128)}, bf16[1024,4608]{1,0:T(8,128)(2,1)}) custom-call(bf16[1152,1024]{1,0:T(8,128)(2,1)} %shard_map.183.o_ref, f32[1024,1152]{1,0:T(8,128)} %get-tuple-element.79.x_ref, f32[6,1152]{1,0:T(8,128)} %get-tuple-element.101.mod_ref, bf16[2,720,1152]{2,1,0:T(8,128)(2,1)} %pad_maximum_fusion.own, ...), custom_call_target="tpu_custom_call" | custom-call | flops 13589544960 | bytes 18874368 | tf_op jit(solution)/shard_map/pallas_call | solution.py:248
  412.2 24.7 %shard_map.185 = f32[16,1024]{1,0:T(8,128)} custom-call(bf16[1024,4608]{1,0:T(8,128)(2,1)} %get-tuple-element.82.u_ref, f32[1024,1152]{1,0:T(8,128)} %get-tuple-element.83.x_ref, f32[6,1152]{1,0:T(8,128)} %get-tuple-element.101.mod_ref, bf16[2,576,1152]{2,1,0:T(8,128)(2,1)} %bitcast.96, bf16[2,576,1152]{2,1,0:T(8,128)(2,1)} %collective-permute-done.37.partner, ...), custom_call_target="tpu_custom_call" | custom-call | flops 10871635968 | bytes 18874368 | tf_op jit(solution)/shard_map/pallas_call | solution.py:289
  436.9 2.7 collective-permute-start.40
  439.6 4.2 collective-permute-done.40
  444.6 5.8 %all-gather = f32[64,1024]{1,0:T(8,128)S(1)} all-gather(f32[16,1024]{1,0:T(8,128)S(1)} %multiply_add_fusion), channel_id=2, replica_groups=mesh['dp'=2,'cfg'=4,'tp'=4] {'tp'}, dimensions={0}, use_global_device_ids=true | all-gather | bytes 327680 | tf_op jit(solution)/shard_map/all_gather | solution.py:399
  451.1 7.9 %collective-permute-done.41 = f32[4,16,1024]{2,1,0:T(8,128)S(1)} collective-permute-done((f32[4,16,1024]{2,1,0:T(8,128)S(1)}, f32[4,16,1024]{2,1,0:T(8,128)S(1)}, u32[]{:S(2)}, u32[]{:S(2)}) %collective-permute-start.41) | collective-permute-done | bytes 262176 | tf_op jit(solution)/shard_map/ppermute | solution.py:400
  459.7 8.9 %copy.60 = f32[8,32,2,32,2,4]{0,4,3,5,2,1:T(2,128)} copy(f32[8,32,2,32,2,4]{3,1,5,4,2,0:T(8,128)S(1)} %bitcast.93) | data formatting | bytes 1048576 | tf_op jit(solution)/shard_map/transpose | solution.py:404
  468.7 5.3 %copy.61 = f32[8,64,64,4]{2,1,3,0:T(8,128)S(1)} copy(f32[8,64,64,4]{0,2,3,1:T(8,128)} %bitcast.92) | data formatting | bytes 1048576 | tf_op jit(solution)/shard_map/reshape | solution.py:404
  474.3 1.6 copy.64
  (154 shorter events, 38.0 us)
Async XLA Ops:
  5.2 57.1 %collective-permute-start.8 = (bf16[2,432,1152]{2,1,0:T(8,128)(2,1)}, bf16[2,432,1152]{2,1,0:T(8,128)(2,1)}, u32[]{:S(2)}, u32[]{:S(2)}) collective-permute-start(bf16[2,432,1152]{2,1,0:T(8,128)(2,1)} %bitcast.34.own), channel_id=1, source_target_pairs={{0,1},{1,0},{2,3},{3,2},{4,5},{5,4},{6,7},{7,6},{8,9},{9,8},{10,11... | collective-permute-start | bytes 5971976 | tf_op jit(solution)/shard_map/ppermute | solution.py:316
  8.0 25.8 %collective-permute-start.6 = (bf16[432,1152]{1,0:T(8,128)(2,1)}, bf16[432,1152]{1,0:T(8,128)(2,1)}, u32[]{:S(2)}, u32[]{:S(2)}) collective-permute-start(bf16[432,1152]{1,0:T(8,128)(2,1)} %dynamic-slice_bitcast_fusion.7), channel_id=1, source_target_pairs={{0,2},{1,3},{2,0},{3,1},{4,6},{5,7},{6,4},{7,5},{8,10},{9,11},{10,... | collective-permute-start | bytes 2985992 | tf_op jit(solution)/shard_map/ppermute | solution.py:315
  17.9 108.8 %collective-permute-start.13 = (bf16[2,720,1152]{2,1,0:T(8,128)(2,1)}, bf16[2,720,1152]{2,1,0:T(8,128)(2,1)}, u32[]{:S(2)}, u32[]{:S(2)}) collective-permute-start(bf16[2,720,1152]{2,1,0:T(8,128)(2,1)} %pad_maximum_fusion.1.own), channel_id=1, source_target_pairs={{0,1},{1,0},{2,3},{3,2},{4,5},{5,4},{6,7},{7,6},{8,9},{9,8},{10,11... | collective-permute-start | bytes 9953288 | tf_op jit(solution)/shard_map/ppermute | solution.py:316
  20.8 59.8 %collective-permute-start.5 = (bf16[720,1152]{1,0:T(8,128)(2,1)}, bf16[720,1152]{1,0:T(8,128)(2,1)}, u32[]{:S(2)}, u32[]{:S(2)}) collective-permute-start(bf16[720,1152]{1,0:T(8,128)(2,1)} %dynamic-slice_bitcast_fusion.1), channel_id=1, source_target_pairs={{0,2},{1,3},{2,0},{3,1},{4,6},{5,7},{6,4},{7,5},{8,10},{9,11},{10,... | collective-permute-start | bytes 4976648 | tf_op jit(solution)/shard_map/ppermute | solution.py:315
  33.7 23.8 %collective-permute-start.7 = (bf16[432,1152]{1,0:T(8,128)(2,1)}, bf16[432,1152]{1,0:T(8,128)(2,1)}, u32[]{:S(2)}, u32[]{:S(2)}) collective-permute-start(bf16[432,1152]{1,0:T(8,128)(2,1)} %collective-permute-done.6.y), channel_id=1, source_target_pairs={{0,16},{16,0},{1,17},{17,1},{2,18},{18,2},{3,19},{19,3},{4,20},{20... | collective-permute-start | bytes 2985992 | tf_op jit(solution)/shard_map/ppermute | solution.py:320
  43.5 17.6 %copy-start.15 = (bf16[2,6,1152]{2,0,1:T(2,128)(2,1)S(1)}, bf16[2,6,1152]{2,0,1:T(2,128)(2,1)}, u32[]{:S(2)}) copy-start(bf16[2,6,1152]{2,0,1:T(2,128)(2,1)} %param.25) | copy-start | bytes 82948
  43.5 18.3 %collective-permute-start.9 = (bf16[432,1152]{1,0:T(8,128)(2,1)}, bf16[432,1152]{1,0:T(8,128)(2,1)S(1)}, u32[]{:S(2)}, u32[]{:S(2)}) collective-permute-start(bf16[432,1152]{1,0:T(8,128)(2,1)} %collective-permute-done.6.y), channel_id=1, source_target_pairs={{0,1},{1,0},{2,3},{3,2},{4,5},{5,4},{6,7},{7,6},{8,9},{9,8},{10,11... | collective-permute-start | bytes 2985992 | tf_op jit(solution)/shard_map/ppermute | solution.py:321
  57.6 6.2 %collective-permute-start.10 = (bf16[432,1152]{1,0:T(8,128)(2,1)}, bf16[432,1152]{1,0:T(8,128)(2,1)S(1)}, u32[]{:S(2)}, u32[]{:S(2)}) collective-permute-start(bf16[432,1152]{1,0:T(8,128)(2,1)} %collective-permute-done.7.x), channel_id=1, source_target_pairs={{0,1},{1,0},{2,3},{3,2},{4,5},{5,4},{6,7},{7,6},{8,9},{9,8},{10,11... | collective-permute-start | bytes 2985992 | tf_op jit(solution)/shard_map/ppermute | solution.py:326
  61.8 106.6 %collective-permute-start.16 = (bf16[2,576,1152]{2,1,0:T(8,128)(2,1)}, bf16[2,576,1152]{2,1,0:T(8,128)(2,1)}, u32[]{:S(2)}, u32[]{:S(2)}) collective-permute-start(bf16[2,576,1152]{2,1,0:T(8,128)(2,1)} %bitcast.21.own1), channel_id=1, source_target_pairs={{0,1},{1,0},{2,3},{3,2},{4,5},{5,4},{6,7},{7,6},{8,9},{9,8},{10,11... | collective-permute-start | bytes 7962632 | tf_op jit(solution)/shard_map/ppermute | solution.py:316
  62.3 54.3 %collective-permute-start.4 = (bf16[576,1152]{1,0:T(8,128)(2,1)}, bf16[576,1152]{1,0:T(8,128)(2,1)}, u32[]{:S(2)}, u32[]{:S(2)}) collective-permute-start(bf16[576,1152]{1,0:T(8,128)(2,1)} %dynamic-slice_bitcast_fusion.4), channel_id=1, source_target_pairs={{0,2},{1,3},{2,0},{3,1},{4,6},{5,7},{6,4},{7,5},{8,10},{9,11},{10,... | collective-permute-start | bytes 3981320 | tf_op jit(solution)/shard_map/ppermute | solution.py:315
  80.6 38.2 %collective-permute-start.12 = (bf16[720,1152]{1,0:T(8,128)(2,1)}, bf16[720,1152]{1,0:T(8,128)(2,1)S(1)}, u32[]{:S(2)}, u32[]{:S(2)}) collective-permute-start(bf16[720,1152]{1,0:T(8,128)(2,1)} %collective-permute-done.5.y), channel_id=1, source_target_pairs={{0,16},{16,0},{1,17},{17,1},{2,18},{18,2},{3,19},{19,3},{4,20},{20... | collective-permute-start | bytes 4976648 | tf_op jit(solution)/shard_map/ppermute | solution.py:320
  87.1 40.2 %collective-permute-start.14 = (bf16[720,1152]{1,0:T(8,128)(2,1)}, bf16[720,1152]{1,0:T(8,128)(2,1)}, u32[]{:S(2)}, u32[]{:S(2)}) collective-permute-start(bf16[720,1152]{1,0:T(8,128)(2,1)} %collective-permute-done.5.y), channel_id=1, source_target_pairs={{0,1},{1,0},{2,3},{3,2},{4,5},{5,4},{6,7},{7,6},{8,9},{9,8},{10,11... | collective-permute-start | bytes 4976648 | tf_op jit(solution)/shard_map/ppermute | solution.py:321
  118.9 8.4 %collective-permute-start.15 = (bf16[720,1152]{1,0:T(8,128)(2,1)S(1)}, bf16[720,1152]{1,0:T(8,128)(2,1)}, u32[]{:S(2)}, u32[]{:S(2)}) collective-permute-start(bf16[720,1152]{1,0:T(8,128)(2,1)S(1)} %collective-permute-done.12.x), channel_id=1, source_target_pairs={{0,1},{1,0},{2,3},{3,2},{4,5},{5,4},{6,7},{7,6},{8,9},{9,8},{10,11... | collective-permute-start | bytes 4976648 | tf_op jit(solution)/shard_map/ppermute | solution.py:326
  123.9 41.2 %collective-permute-start.11 = (bf16[576,1152]{1,0:T(8,128)(2,1)}, bf16[576,1152]{1,0:T(8,128)(2,1)}, u32[]{:S(2)}, u32[]{:S(2)}) collective-permute-start(bf16[576,1152]{1,0:T(8,128)(2,1)} %collective-permute-done.4.y1), channel_id=1, source_target_pairs={{0,16},{16,0},{1,17},{17,1},{2,18},{18,2},{3,19},{19,3},{4,20},{20... | collective-permute-start | bytes 3981320 | tf_op jit(solution)/shard_map/ppermute | solution.py:320
  126.7 39.2 %collective-permute-start.3 = (bf16[576,1152]{1,0:T(8,128)(2,1)}, bf16[576,1152]{1,0:T(8,128)(2,1)}, u32[]{:S(2)}, u32[]{:S(2)}) collective-permute-start(bf16[576,1152]{1,0:T(8,128)(2,1)} %dynamic-slice_bitcast_fusion.5), channel_id=1, source_target_pairs={{0,2},{1,3},{2,0},{3,1},{4,6},{5,7},{6,4},{7,5},{8,10},{9,11},{10,... | collective-permute-start | bytes 3981320 | tf_op jit(solution)/shard_map/ppermute | solution.py:315
  127.3 42.6 %collective-permute-start.17 = (bf16[576,1152]{1,0:T(8,128)(2,1)}, bf16[576,1152]{1,0:T(8,128)(2,1)}, u32[]{:S(2)}, u32[]{:S(2)}) collective-permute-start(bf16[576,1152]{1,0:T(8,128)(2,1)} %collective-permute-done.4.y1), channel_id=1, source_target_pairs={{0,1},{1,0},{2,3},{3,2},{4,5},{5,4},{6,7},{7,6},{8,9},{9,8},{10,11... | collective-permute-start | bytes 3981320 | tf_op jit(solution)/shard_map/ppermute | solution.py:321
  165.2 4.8 %collective-permute-start.18 = (bf16[576,1152]{1,0:T(8,128)(2,1)}, bf16[576,1152]{1,0:T(8,128)(2,1)S(1)}, u32[]{:S(2)}, u32[]{:S(2)}) collective-permute-start(bf16[576,1152]{1,0:T(8,128)(2,1)} %collective-permute-done.11.x1), channel_id=1, source_target_pairs={{0,1},{1,0},{2,3},{3,2},{4,5},{5,4},{6,7},{7,6},{8,9},{9,8},{10,11... | collective-permute-start | bytes 3981320 | tf_op jit(solution)/shard_map/ppermute | solution.py:326
  165.6 42.4 %collective-permute-start.21 = (bf16[2,576,1152]{2,1,0:T(8,128)(2,1)}, bf16[2,576,1152]{2,1,0:T(8,128)(2,1)}, u32[]{:S(2)}, u32[]{:S(2)}) collective-permute-start(bf16[2,576,1152]{2,1,0:T(8,128)(2,1)} %bitcast.98), channel_id=1, source_target_pairs={{0,1},{1,0},{2,3},{3,2},{4,5},{5,4},{6,7},{7,6},{8,9},{9,8},{10,11... | collective-permute-start | bytes 7962632 | tf_op jit(solution)/shard_map/ppermute | solution.py:316
  165.9 38.2 %collective-permute-start.20 = (bf16[576,1152]{1,0:T(8,128)(2,1)}, bf16[576,1152]{1,0:T(8,128)(2,1)}, u32[]{:S(2)}, u32[]{:S(2)}) collective-permute-start(bf16[576,1152]{1,0:T(8,128)(2,1)} %collective-permute-done.3.y), channel_id=1, source_target_pairs={{0,16},{16,0},{1,17},{17,1},{2,18},{18,2},{3,19},{19,3},{4,20},{20... | collective-permute-start | bytes 3981320 | tf_op jit(solution)/shard_map/ppermute | solution.py:320
  168.4 35.7 %collective-permute-start.2 = (bf16[432,1152]{1,0:T(8,128)(2,1)}, bf16[432,1152]{1,0:T(8,128)(2,1)}, u32[]{:S(2)}, u32[]{:S(2)}) collective-permute-start(bf16[432,1152]{1,0:T(8,128)(2,1)} %dynamic-slice_bitcast_fusion.8), channel_id=1, source_target_pairs={{0,2},{1,3},{2,0},{3,1},{4,6},{5,7},{6,4},{7,5},{8,10},{9,11},{10,... | collective-permute-start | bytes 2985992 | tf_op jit(solution)/shard_map/ppermute | solution.py:315
  169.9 38.3 %collective-permute-start.22 = (bf16[576,1152]{1,0:T(8,128)(2,1)}, bf16[576,1152]{1,0:T(8,128)(2,1)}, u32[]{:S(2)}, u32[]{:S(2)}) collective-permute-start(bf16[576,1152]{1,0:T(8,128)(2,1)} %collective-permute-done.3.y), channel_id=1, source_target_pairs={{0,1},{1,0},{2,3},{3,2},{4,5},{5,4},{6,7},{7,6},{8,9},{9,8},{10,11... | collective-permute-start | bytes 3981320 | tf_op jit(solution)/shard_map/ppermute | solution.py:321
  171.0 33.7 %copy-start.4 = (bf16[4,2,72,1152]{3,2,0,1:T(8,128)(2,1)S(1)}, bf16[4,2,72,1152]{3,2,0,1:T(8,128)(2,1)}, u32[]{:S(2)}) copy-start(bf16[4,2,72,1152]{3,2,0,1:T(8,128)(2,1)} %get-tuple-element.92) | copy-start | bytes 3981316
  204.1 4.1 collective-permute-start.23
  204.7 34.6 %collective-permute-start.24 = (bf16[2,432,1152]{2,1,0:T(8,128)(2,1)}, bf16[2,432,1152]{2,1,0:T(8,128)(2,1)}, u32[]{:S(2)}, u32[]{:S(2)}) collective-permute-start(bf16[2,432,1152]{2,1,0:T(8,128)(2,1)} %bitcast.103), channel_id=1, source_target_pairs={{0,1},{1,0},{2,3},{3,2},{4,5},{5,4},{6,7},{7,6},{8,9},{9,8},{10,11... | collective-permute-start | bytes 5971976 | tf_op jit(solution)/shard_map/ppermute | solution.py:316
  207.4 24.7 %collective-permute-start.19 = (bf16[432,1152]{1,0:T(8,128)(2,1)}, bf16[432,1152]{1,0:T(8,128)(2,1)}, u32[]{:S(2)}, u32[]{:S(2)}) collective-permute-start(bf16[432,1152]{1,0:T(8,128)(2,1)} %collective-permute-done.2.y), channel_id=1, source_target_pairs={{0,16},{16,0},{1,17},{17,1},{2,18},{18,2},{3,19},{19,3},{4,20},{20... | collective-permute-start | bytes 2985992 | tf_op jit(solution)/shard_map/ppermute | solution.py:320
  208.1 31.2 %collective-permute-start.25 = (bf16[432,1152]{1,0:T(8,128)(2,1)}, bf16[432,1152]{1,0:T(8,128)(2,1)}, u32[]{:S(2)}, u32[]{:S(2)}) collective-permute-start(bf16[432,1152]{1,0:T(8,128)(2,1)} %collective-permute-done.2.y), channel_id=1, source_target_pairs={{0,1},{1,0},{2,3},{3,2},{4,5},{5,4},{6,7},{7,6},{8,9},{9,8},{10,11... | collective-permute-start | bytes 2985992 | tf_op jit(solution)/shard_map/ppermute | solution.py:321
  232.2 7.1 %collective-permute-start.26 = (bf16[432,1152]{1,0:T(8,128)(2,1)}, bf16[432,1152]{1,0:T(8,128)(2,1)}, u32[]{:S(2)}, u32[]{:S(2)}) collective-permute-start(bf16[432,1152]{1,0:T(8,128)(2,1)} %collective-permute-done.19.x), channel_id=1, source_target_pairs={{0,1},{1,0},{2,3},{3,2},{4,5},{5,4},{6,7},{7,6},{8,9},{9,8},{10,11... | collective-permute-start | bytes 2985992 | tf_op jit(solution)/shard_map/ppermute | solution.py:326
  235.1 38.9 %collective-permute-start.1 = (bf16[720,1152]{1,0:T(8,128)(2,1)}, bf16[720,1152]{1,0:T(8,128)(2,1)}, u32[]{:S(2)}, u32[]{:S(2)}) collective-permute-start(bf16[720,1152]{1,0:T(8,128)(2,1)} %dynamic-slice_bitcast_fusion.2), channel_id=1, source_target_pairs={{0,2},{1,3},{2,0},{3,1},{4,6},{5,7},{6,4},{7,5},{8,10},{9,11},{10,... | collective-permute-start | bytes 4976648 | tf_op jit(solution)/shard_map/ppermute | solution.py:315
  235.9 80.4 %collective-permute-start.29 = (bf16[2,720,1152]{2,1,0:T(8,128)(2,1)}, bf16[2,720,1152]{2,1,0:T(8,128)(2,1)}, u32[]{:S(2)}, u32[]{:S(2)}) collective-permute-start(bf16[2,720,1152]{2,1,0:T(8,128)(2,1)} %pad_maximum_fusion.own), channel_id=1, source_target_pairs={{0,1},{1,0},{2,3},{3,2},{4,5},{5,4},{6,7},{7,6},{8,9},{9,8},{10,11... | collective-permute-start | bytes 9953288 | tf_op jit(solution)/shard_map/ppermute | solution.py:316
  274.0 37.9 %collective-permute-start.27 = (bf16[720,1152]{1,0:T(8,128)(2,1)}, bf16[720,1152]{1,0:T(8,128)(2,1)S(1)}, u32[]{:S(2)}, u32[]{:S(2)}) collective-permute-start(bf16[720,1152]{1,0:T(8,128)(2,1)} %collective-permute-done.1.y), channel_id=1, source_target_pairs={{0,16},{16,0},{1,17},{17,1},{2,18},{18,2},{3,19},{19,3},{4,20},{20... | collective-permute-start | bytes 4976648 | tf_op jit(solution)/shard_map/ppermute | solution.py:320
  277.6 30.4 %collective-permute-start.28 = (bf16[576,1152]{1,0:T(8,128)(2,1)}, bf16[576,1152]{1,0:T(8,128)(2,1)}, u32[]{:S(2)}, u32[]{:S(2)}) collective-permute-start(bf16[576,1152]{1,0:T(8,128)(2,1)} %dynamic-slice_bitcast_fusion.3), channel_id=1, source_target_pairs={{0,2},{1,3},{2,0},{3,1},{4,6},{5,7},{6,4},{7,5},{8,10},{9,11},{10,... | collective-permute-start | bytes 3981320 | tf_op jit(solution)/shard_map/ppermute | solution.py:315
  278.1 38.3 %collective-permute-start.30 = (bf16[720,1152]{1,0:T(8,128)(2,1)}, bf16[720,1152]{1,0:T(8,128)(2,1)}, u32[]{:S(2)}, u32[]{:S(2)}) collective-permute-start(bf16[720,1152]{1,0:T(8,128)(2,1)} %collective-permute-done.1.y), channel_id=1, source_target_pairs={{0,1},{1,0},{2,3},{3,2},{4,5},{5,4},{6,7},{7,6},{8,9},{9,8},{10,11... | collective-permute-start | bytes 4976648 | tf_op jit(solution)/shard_map/ppermute | solution.py:321
  311.9 5.0 %collective-permute-start.31 = (bf16[720,1152]{1,0:T(8,128)(2,1)S(1)}, bf16[720,1152]{1,0:T(8,128)(2,1)}, u32[]{:S(2)}, u32[]{:S(2)}) collective-permute-start(bf16[720,1152]{1,0:T(8,128)(2,1)S(1)} %collective-permute-done.27.x), channel_id=1, source_target_pairs={{0,1},{1,0},{2,3},{3,2},{4,5},{5,4},{6,7},{7,6},{8,9},{9,8},{10,11... | collective-permute-start | bytes 4976648 | tf_op jit(solution)/shard_map/ppermute | solution.py:326
  315.0 31.3 %collective-permute-start = (bf16[576,1152]{1,0:T(8,128)(2,1)}, bf16[576,1152]{1,0:T(8,128)(2,1)}, u32[]{:S(2)}, u32[]{:S(2)}) collective-permute-start(bf16[576,1152]{1,0:T(8,128)(2,1)} %dynamic-slice_bitcast_fusion.6), channel_id=1, source_target_pairs={{0,2},{1,3},{2,0},{3,1},{4,6},{5,7},{6,4},{7,5},{8,10},{9,11},{10,... | collective-permute-start | bytes 3981320 | tf_op jit(solution)/shard_map/ppermute | solution.py:315
  315.7 54.2 %collective-permute-start.33 = (bf16[576,1152]{1,0:T(8,128)(2,1)}, bf16[576,1152]{1,0:T(8,128)(2,1)}, u32[]{:S(2)}, u32[]{:S(2)}) collective-permute-start(bf16[576,1152]{1,0:T(8,128)(2,1)} %collective-permute-done.28.y1), channel_id=1, source_target_pairs={{0,16},{16,0},{1,17},{17,1},{2,18},{18,2},{3,19},{19,3},{4,20},{20... | collective-permute-start | bytes 3981320 | tf_op jit(solution)/shard_map/ppermute | solution.py:320
  316.4 54.6 %collective-permute-start.34 = (bf16[2,576,1152]{2,1,0:T(8,128)(2,1)}, bf16[2,576,1152]{2,1,0:T(8,128)(2,1)}, u32[]{:S(2)}, u32[]{:S(2)}) collective-permute-start(bf16[2,576,1152]{2,1,0:T(8,128)(2,1)} %bitcast.42.own1), channel_id=1, source_target_pairs={{0,1},{1,0},{2,3},{3,2},{4,5},{5,4},{6,7},{7,6},{8,9},{9,8},{10,11... | collective-permute-start | bytes 7962632 | tf_op jit(solution)/shard_map/ppermute | solution.py:316
  316.4 55.0 %collective-permute-start.35 = (bf16[576,1152]{1,0:T(8,128)(2,1)}, bf16[576,1152]{1,0:T(8,128)(2,1)}, u32[]{:S(2)}, u32[]{:S(2)}) collective-permute-start(bf16[576,1152]{1,0:T(8,128)(2,1)} %collective-permute-done.28.y1), channel_id=1, source_target_pairs={{0,1},{1,0},{2,3},{3,2},{4,5},{5,4},{6,7},{7,6},{8,9},{9,8},{10,11... | collective-permute-start | bytes 3981320 | tf_op jit(solution)/shard_map/ppermute | solution.py:321
  369.9 3.3 collective-permute-start.36
  369.9 37.4 %collective-permute-start.32 = (bf16[576,1152]{1,0:T(8,128)(2,1)}, bf16[576,1152]{1,0:T(8,128)(2,1)S(1)}, u32[]{:S(2)}, u32[]{:S(2)}) collective-permute-start(bf16[576,1152]{1,0:T(8,128)(2,1)} %collective-permute-done.y), channel_id=1, source_target_pairs={{0,16},{16,0},{1,17},{17,1},{2,18},{18,2},{3,19},{19,3},{4,20},{20... | collective-permute-start | bytes 3981320 | tf_op jit(solution)/shard_map/ppermute | solution.py:320
  370.8 39.1 %collective-permute-start.37 = (bf16[2,576,1152]{2,1,0:T(8,128)(2,1)}, bf16[2,576,1152]{2,1,0:T(8,128)(2,1)}, u32[]{:S(2)}, u32[]{:S(2)}) collective-permute-start(bf16[2,576,1152]{2,1,0:T(8,128)(2,1)} %bitcast.95), channel_id=1, source_target_pairs={{0,1},{1,0},{2,3},{3,2},{4,5},{5,4},{6,7},{7,6},{8,9},{9,8},{10,11... | collective-permute-start | bytes 7962632 | tf_op jit(solution)/shard_map/ppermute | solution.py:316
  371.0 38.9 %collective-permute-start.38 = (bf16[576,1152]{1,0:T(8,128)(2,1)}, bf16[576,1152]{1,0:T(8,128)(2,1)}, u32[]{:S(2)}, u32[]{:S(2)}) collective-permute-start(bf16[576,1152]{1,0:T(8,128)(2,1)} %collective-permute-done.y), channel_id=1, source_target_pairs={{0,1},{1,0},{2,3},{3,2},{4,5},{5,4},{6,7},{7,6},{8,9},{9,8},{10,11... | collective-permute-start | bytes 3981320 | tf_op jit(solution)/shard_map/ppermute | solution.py:321
  374.3 33.2 %copy-start.16 = (bf16[1152,32]{0,1:T(8,128)(2,1)S(1)}, bf16[1152,32]{0,1:T(8,128)(2,1)}, u32[]{:S(2)}) copy-start(bf16[1152,32]{0,1:T(8,128)(2,1)} %param.34) | copy-start | bytes 221188
  374.3 34.1 %copy-start.26 = (bf16[32]{0:T(256)(128)(2,1)S(1)}, bf16[32]{0:T(256)(128)(2,1)}, u32[]{:S(2)}) copy-start(bf16[32]{0:T(256)(128)(2,1)} %param.35) | copy-start | bytes 196
  374.3 35.0 %copy-start.17 = (bf16[2,1152]{1,0:T(2,128)(2,1)S(1)}, bf16[2,1152]{1,0:T(2,128)(2,1)}, u32[]{:S(2)}) copy-start(bf16[2,1152]{1,0:T(2,128)(2,1)} %param.33) | copy-start | bytes 13828
  407.3 3.1 collective-permute-start.39
  412.2 38.9 %copy-start.18 = (f32[8,2]{0,1:T(2,128)S(1)}, f32[8,2]{0,1:T(2,128)}, u32[]{:S(2)}) copy-start(f32[8,2]{0,1:T(2,128)} %param.24) | copy-start | bytes 196
  436.9 6.8 %collective-permute-start.40 = (f32[16,1024]{1,0:T(8,128)}, f32[16,1024]{1,0:T(8,128)S(1)}, u32[]{:S(2)}, u32[]{:S(2)}) collective-permute-start(f32[16,1024]{1,0:T(8,128)} %shard_map.185), channel_id=1, source_target_pairs={{0,8},{4,12},{8,0},{12,4},{1,9},{5,13},{9,1},{13,5},{2,10},{6,14},... | collective-permute-start | bytes 196616 | tf_op jit(solution)/shard_map/ppermute | solution.py:394
  450.4 8.6 %collective-permute-start.41 = (f32[4,16,1024]{2,1,0:T(8,128)S(1)}, f32[4,16,1024]{2,1,0:T(8,128)S(1)}, u32[]{:S(2)}, u32[]{:S(2)}) collective-permute-start(f32[4,16,1024]{2,1,0:T(8,128)S(1)} %bitcast.112), channel_id=1, source_target_pairs={{0,4},{4,0},{8,12},{12,8},{1,5},{5,1},{9,13},{13,9},{2,6},{6,2},{1... | collective-permute-start | bytes 786440 | tf_op jit(solution)/shard_map/ppermute | solution.py:400
  (21 other events, 74.2 us)
